TPU v7x, 128 devices: a whole 4x4x4 slice. The times are simulated.
128 devices in a mesh: ctx: 32 (over y, z, core), head: 4 (over x).
Axes of the slice: x: 4, y: 4, z: 4, core: 2. Of those that a mesh axis runs over, the one named last changes fastest.
Arguments:
- queries: bfloat16 [32, 32768, 128], P('head', 'ctx'), may hold values from -0.52734375 to 0.52734375
- key_rows: bfloat16 [32, 32768, 128], P('head', 'ctx'), may hold values from -0.52734375 to 0.52734375
- value_rows: bfloat16 [32, 32768, 128], P('head', 'ctx'), may hold values from -0.52734375 to 0.52734375
- level_weight: float32 [6, 32768], P(None, 'ctx'), may hold values from 0.2 to 2
- out_grad: bfloat16 [32, 32768, 128], P('head', 'ctx'), may hold values from -0.52734375 to 0.52734375
Outputs:
- query_grad: bfloat16 [32, 32768, 128], P('head', 'ctx')
- key_grad: bfloat16 [32, 32768, 128], P('head', 'ctx')
- value_grad: bfloat16 [32, 32768, 128], P('head', 'ctx')
- weight_grad: float32 [6, 32768], P(None, 'ctx')
All inputs are finite; a program needn't handle non-finite values.
Results may differ from a plain program's by a relative error of at most 0.0057.
Values sent between devices are 32-bit elements; how exact they have to be, the bound alone decides.
A program may use at most 128 MiB of HBM per device.

v0:
```python
import jax
import jax.numpy as jnp
from jax import lax
from jax.sharding import PartitionSpec as P


def partner_2(shard, axis, distance):
    return lax.ppermute(shard, axis, [(i, i ^ 1 << distance) for i in range(lax.axis_size(axis))])


def local_block(operands, first_weight):
    queries, key_rows, value_rows, out_grad = operands
    length = queries.shape[0]
    steps = jnp.arange(length, dtype=jnp.int32)
    causal = (steps[:, None] >= steps[None, :]).astype(jnp.float32)
    scale = causal * first_weight[:, None]
    raw = jnp.einsum("td,sd->ts", queries, key_rows, preferred_element_type=jnp.float32)
    attn = (scale * raw).astype(jnp.bfloat16)
    d_attn = jnp.einsum("td,sd->ts", out_grad, value_rows, preferred_element_type=jnp.float32)
    local_weight = jnp.sum(causal * raw * d_attn, axis=1)
    d_raw = (scale * d_attn).astype(jnp.bfloat16)
    local_q = jnp.einsum("ts,sd->td", d_raw, key_rows, preferred_element_type=jnp.float32)
    local_k = jnp.einsum("ts,td->sd", d_raw, queries, preferred_element_type=jnp.float32)
    local_v = jnp.einsum("ts,td->sd", attn, out_grad, preferred_element_type=jnp.float32)
    return (local_q, local_k, local_v, local_weight)


def per_device(queries, key_rows, value_rows, level_weight, out_grad):
    levels = lax.axis_size("ctx").bit_length() - 1
    position = lax.axis_index("ctx")
    bit_flags = [(position // 2**height % 2).astype(jnp.float32) for height in range(levels)]
    group_state = jnp.einsum(
        "hcd,hce->hde", key_rows, value_rows, preferred_element_type=jnp.float32
    )
    pending = []
    for height in range(levels):
        level_row = level_weight[height + 1]
        weighted = (level_row[None, :, None] * out_grad.astype(jnp.float32)).astype(jnp.bfloat16)
        state_grad = jnp.einsum(
            "htd,hte->hde", queries, weighted, preferred_element_type=jnp.float32
        )
        pending.append(bit_flags[height] * state_grad)
    group_grad = jnp.zeros(group_state.shape, jnp.float32)
    running = group_state
    states = []
    for height in range(levels):
        partner = partner_2(running, "ctx", height)
        states.append(bit_flags[height] * partner)
        running = running + partner
    local_q, local_k, local_v, local_weight = lax.map(
        lambda operands: local_block(operands, level_weight[0]),
        (queries, key_rows, value_rows, out_grad),
    )
    query_sum = local_q
    q_float = queries.astype(jnp.float32)
    weight_rows = [jnp.sum(local_weight, axis=0)]
    for height in range(levels):
        state_bf = states[height].astype(jnp.bfloat16)
        level_row = level_weight[height + 1]
        z_part = jnp.einsum("hte,hde->htd", out_grad, state_bf, preferred_element_type=jnp.float32)
        query_sum = query_sum + level_row[None, :, None] * z_part
        weight_rows.append(jnp.sum(z_part * q_float, axis=(0, 2)))
    weight_grad = lax.psum(jnp.stack(weight_rows, axis=0), "head")
    for section_no in range(levels):
        received = partner_2(jnp.stack(pending[section_no:], axis=0), "ctx", section_no)
        group_grad = group_grad + (1.0 - bit_flags[section_no]) * received[0]
        for later in range(section_no + 1, levels):
            pending[later] = pending[later] + received[later - section_no]
    grad_bf = group_grad.astype(jnp.bfloat16)
    key_sum = local_k + jnp.einsum(
        "hse,hde->hsd", value_rows, grad_bf, preferred_element_type=jnp.float32
    )
    value_sum = local_v + jnp.einsum(
        "hsd,hde->hse", key_rows, grad_bf, preferred_element_type=jnp.float32
    )
    return (
        query_sum.astype(jnp.bfloat16),
        key_sum.astype(jnp.bfloat16),
        value_sum.astype(jnp.bfloat16),
        weight_grad,
    )


def solution(mesh):
    placed = (
        P("head", "ctx", None),
        P("head", "ctx", None),
        P("head", "ctx", None),
        P(None, "ctx"),
        P("head", "ctx", None),
    )
    return jax.shard_map(
        per_device,
        mesh=mesh,
        in_specs=placed,
        out_specs=(
            P("head", "ctx", None),
            P("head", "ctx", None),
            P("head", "ctx", None),
            P(None, "ctx"),
        ),
        check_vma=False,
    )
```

profile of v0, /device:TPU:0, one launch (start us, length us, event | category | flops | bytes accessed | tf_op | source)
XLA Modules:
  0.0 298.8 jit_solution(12998476130922800051)
XLA Ops:
  1.7 3.9 %copy.11 = bf16[8,1024,128]{1,2,0:T(8,128)(2,1)} copy(bf16[8,1024,128]{2,1,0:T(8,128)(2,1)} %param.11) | data formatting | bytes 4194304 | tf_op args[4]
  11.2 4.9 %collective-permute-done.5 = f32[5,8,128,128]{2,3,1,0:T(8,128)S(1)} collective-permute-done((f32[5,8,128,128]{2,3,1,0:T(8,128)S(1)}, f32[5,8,128,128]{2,3,1,0:T(8,128)S(1)}, u32[]{:S(2)}, u32[]{:S(2)}) %collective-permute-start.5) | collective-permute-done | bytes 2621472 | tf_op jit(solution)/shard_map/ppermute | solution.py:8
  25.6 51.8 %collective-permute-done.1 = f32[8,128,128]{2,1,0:T(8,128)} collective-permute-done((f32[8,128,128]{2,1,0:T(8,128)S(1)}, f32[8,128,128]{2,1,0:T(8,128)}, u32[]{:S(2)}, u32[]{:S(2)}) %collective-permute-start.1) | collective-permute-done | bytes 524320 | tf_op jit(solution)/shard_map/ppermute | solution.py:8
  79.2 3.7 %collective-permute-start.2 = (f32[8,128,128]{2,1,0:T(8,128)}, f32[8,128,128]{2,1,0:T(8,128)}, u32[]{:S(2)}, u32[]{:S(2)}) collective-permute-start(f32[8,128,128]{2,1,0:T(8,128)} %add.112), channel_id=1, source_target_pairs={{0,16},{4,20},{8,24},{12,28},{16,0},{20,4},{24,8},{28,12},{32,48},... | collective-permute-start | bytes 1572872 | tf_op jit(solution)/shard_map/ppermute | solution.py:8
  87.3 106.2 %while.16 = (s32[]{:T(128)}, f32[8,1024,128]{1,2,0:T(8,128)}, f32[8,1024,128]{1,2,0:T(8,128)}, f32[8,1024,128]{1,2,0:T(8,128)}, f32[8,1024]{1,0:T(8,128)S(1)}, /...) while((s32[]{:T(128)}, f32[8,1024,128]{1,2,0:T(8,128)}, ...), condition=%wide.region_2.3_spmd, body=%wide.region_0.2_spmd.sunk | while | flops 1358953472 | bytes 45388948 | solution.py:50
  96.7 3.9 %fusion.169 = f32[8,1024,128]{1,2,0:T(8,128)} fusion(f32[8,1024,128]{1,2,0:T(8,128)} %get-tuple-element.197, s32[]{:T(128)} %get-tuple-element.194, f32[1024,1024]{0,1:T(8,128)} %copy-done, f32[1024]{0:T(1024)S(1)} %bitcast.273, bf16[8,1024,128]{2,1,0:T(8,128)(2,1)S(1)} %get-tuple-element.212), kind=kOutput, calls=%fused_computation.10.clone.1 | convolution fusion | flops 272629760 | bytes 4985856 | tf_op jit(solution)/shard_map/while/body/eval_jaxpr/ts,td->sd/dot_general | solution.py:24
  110.0 3.9 %fusion.169 = f32[8,1024,128]{1,2,0:T(8,128)} fusion(f32[8,1024,128]{1,2,0:T(8,128)} %get-tuple-element.197, s32[]{:T(128)} %get-tuple-element.194, f32[1024,1024]{0,1:T(8,128)} %copy-done, f32[1024]{0:T(1024)S(1)} %bitcast.273, bf16[8,1024,128]{2,1,0:T(8,128)(2,1)S(1)} %get-tuple-element.212), kind=kOutput, calls=%fused_computation.10.clone.1 | convolution fusion | flops 272629760 | bytes 4985856 | tf_op jit(solution)/shard_map/while/body/eval_jaxpr/ts,td->sd/dot_general | solution.py:24
  123.3 3.8 %fusion.169 = f32[8,1024,128]{1,2,0:T(8,128)} fusion(f32[8,1024,128]{1,2,0:T(8,128)} %get-tuple-element.197, s32[]{:T(128)} %get-tuple-element.194, f32[1024,1024]{0,1:T(8,128)} %copy-done, f32[1024]{0:T(1024)S(1)} %bitcast.273, bf16[8,1024,128]{2,1,0:T(8,128)(2,1)S(1)} %get-tuple-element.212), kind=kOutput, calls=%fused_computation.10.clone.1 | convolution fusion | flops 272629760 | bytes 4985856 | tf_op jit(solution)/shard_map/while/body/eval_jaxpr/ts,td->sd/dot_general | solution.py:24
  136.6 3.8 %fusion.169 = f32[8,1024,128]{1,2,0:T(8,128)} fusion(f32[8,1024,128]{1,2,0:T(8,128)} %get-tuple-element.197, s32[]{:T(128)} %get-tuple-element.194, f32[1024,1024]{0,1:T(8,128)} %copy-done, f32[1024]{0:T(1024)S(1)} %bitcast.273, bf16[8,1024,128]{2,1,0:T(8,128)(2,1)S(1)} %get-tuple-element.212), kind=kOutput, calls=%fused_computation.10.clone.1 | convolution fusion | flops 272629760 | bytes 4985856 | tf_op jit(solution)/shard_map/while/body/eval_jaxpr/ts,td->sd/dot_general | solution.py:24
  149.9 3.8 %fusion.169 = f32[8,1024,128]{1,2,0:T(8,128)} fusion(f32[8,1024,128]{1,2,0:T(8,128)} %get-tuple-element.197, s32[]{:T(128)} %get-tuple-element.194, f32[1024,1024]{0,1:T(8,128)} %copy-done, f32[1024]{0:T(1024)S(1)} %bitcast.273, bf16[8,1024,128]{2,1,0:T(8,128)(2,1)S(1)} %get-tuple-element.212), kind=kOutput, calls=%fused_computation.10.clone.1 | convolution fusion | flops 272629760 | bytes 4985856 | tf_op jit(solution)/shard_map/while/body/eval_jaxpr/ts,td->sd/dot_general | solution.py:24
  163.1 3.8 %fusion.169 = f32[8,1024,128]{1,2,0:T(8,128)} fusion(f32[8,1024,128]{1,2,0:T(8,128)} %get-tuple-element.197, s32[]{:T(128)} %get-tuple-element.194, f32[1024,1024]{0,1:T(8,128)} %copy-done, f32[1024]{0:T(1024)S(1)} %bitcast.273, bf16[8,1024,128]{2,1,0:T(8,128)(2,1)S(1)} %get-tuple-element.212), kind=kOutput, calls=%fused_computation.10.clone.1 | convolution fusion | flops 272629760 | bytes 4985856 | tf_op jit(solution)/shard_map/while/body/eval_jaxpr/ts,td->sd/dot_general | solution.py:24
  176.4 3.8 %fusion.169 = f32[8,1024,128]{1,2,0:T(8,128)} fusion(f32[8,1024,128]{1,2,0:T(8,128)} %get-tuple-element.197, s32[]{:T(128)} %get-tuple-element.194, f32[1024,1024]{0,1:T(8,128)} %copy-done, f32[1024]{0:T(1024)S(1)} %bitcast.273, bf16[8,1024,128]{2,1,0:T(8,128)(2,1)S(1)} %get-tuple-element.212), kind=kOutput, calls=%fused_computation.10.clone.1 | convolution fusion | flops 272629760 | bytes 4985856 | tf_op jit(solution)/shard_map/while/body/eval_jaxpr/ts,td->sd/dot_general | solution.py:24
  189.7 3.8 %fusion.169 = f32[8,1024,128]{1,2,0:T(8,128)} fusion(f32[8,1024,128]{1,2,0:T(8,128)} %get-tuple-element.197, s32[]{:T(128)} %get-tuple-element.194, f32[1024,1024]{0,1:T(8,128)} %copy-done, f32[1024]{0:T(1024)S(1)} %bitcast.273, bf16[8,1024,128]{2,1,0:T(8,128)(2,1)S(1)} %get-tuple-element.212), kind=kOutput, calls=%fused_computation.10.clone.1 | convolution fusion | flops 272629760 | bytes 4985856 | tf_op jit(solution)/shard_map/while/body/eval_jaxpr/ts,td->sd/dot_general | solution.py:24
  193.5 3.9 %copy.15 = bf16[8,1024,128]{1,2,0:T(8,128)(2,1)} copy(bf16[8,1024,128]{2,1,0:T(8,128)(2,1)} %get-tuple-element.222) | data formatting | bytes 4194304 | tf_op args[0]
  208.2 7.4 %collective-permute-done.3 = f32[8,128,128]{2,1,0:T(8,128)S(1)} collective-permute-done((f32[8,128,128]{2,1,0:T(8,128)S(1)}, f32[8,128,128]{2,1,0:T(8,128)S(1)}, u32[]{:S(2)}, u32[]{:S(2)}) %collective-permute-start.3) | collective-permute-done | bytes 524320 | tf_op jit(solution)/shard_map/ppermute | solution.py:8
  221.5 16.5 %collective-permute-done.8 = f32[2,8,128,128]{2,3,1,0:T(8,128)S(1)} collective-permute-done((f32[2,8,128,128]{2,3,1,0:T(8,128)S(1)}, f32[2,8,128,128]{2,3,1,0:T(8,128)S(1)}, u32[]{:S(2)}, u32[]{:S(2)}) %collective-permute-start.8) | collective-permute-done | bytes 1048608 | tf_op jit(solution)/shard_map/ppermute | solution.py:8
  243.5 8.2 %collective-permute-done.4 = f32[8,128,128]{2,1,0:T(8,128)S(1)} collective-permute-done((f32[8,128,128]{2,1,0:T(8,128)S(1)}, f32[8,128,128]{2,1,0:T(8,128)S(1)}, u32[]{:S(2)}, u32[]{:S(2)}) %collective-permute-start.4) | collective-permute-done | bytes 524320 | tf_op jit(solution)/shard_map/ppermute | solution.py:8
  251.7 7.1 %fusion.49 = (f32[1024]{0:T(1024)S(1)}, f32[1024]{0:T(1024)S(1)}, f32[1024]{0:T(1024)S(1)}, f32[1024]{0:T(1024)S(1)}, f32[1024]{0:T(1024)S(1)}, /*index=5*/bf16[8,1024,128]{1,2,0:T(8,128)(2,1)}) fusion(bf16[8,1024,128]{1,2,0:T(8,128)(2,1)S(1)} %copy-done.7, f32[8,128,1024]{2,1,0:T(8,128)S(1)} %fusion.114, f32[8,128,1024]{2,1,0:T(8,128)S(1)} %fusion.115, ...), kind=kOutput, calls=%fused_computation.58 | convolution fusion | flops 291761152 | bytes 27828228 | tf_op jit(solution)/shard_map/hte,hde->htd/dot_general | solution.py:60
  258.8 4.1 %copy.16 = bf16[8,1024,128]{2,1,0:T(8,128)(2,1)} copy(bf16[8,1024,128]{1,2,0:T(8,128)(2,1)} %get-tuple-element.94) | data formatting | bytes 4194304
  262.9 17.7 %psum.7 = f32[6,1024]{1,0:T(8,128)} all-reduce(f32[6,1024]{1,0:T(8,128)S(1)} %stack.103), channel_id=1, replica_groups=mesh['ctx'=32,'head'=4] {'head'}, use_global_device_ids=true, to_apply=%region_9.10 | all-reduce | flops 6144 | bytes 49152 | tf_op jit(solution)/shard_map/psum | solution.py:63
  282.3 4.2 %fusion.50 = bf16[8,1024,128]{1,2,0:T(8,128)(2,1)} fusion(f32[8,1024,128]{1,2,0:T(8,128)} %get-tuple-element.61, bf16[8,1024,128]{2,1,0:T(8,128)(2,1)S(1)} %copy-done.3, bf16[1,8,128,128]{2,3,1,0:T(8,128)(2,1)S(1)} %fusion.98), kind=kOutput, calls=%fused_computation.60 | convolution fusion | flops 270532608 | bytes 8650752 | tf_op jit(solution)/shard_map/hsd,hde->hse/dot_general | solution.py:73
  286.6 4.1 %copy.18 = bf16[8,1024,128]{2,1,0:T(8,128)(2,1)} copy(bf16[8,1024,128]{1,2,0:T(8,128)(2,1)} %fusion.50) | data formatting | bytes 4194304
  290.6 4.3 %fusion.51 = bf16[8,1024,128]{1,2,0:T(8,128)(2,1)} fusion(f32[8,1024,128]{1,2,0:T(8,128)} %get-tuple-element.60, bf16[8,1024,128]{2,1,0:T(8,128)(2,1)S(1)} %copy-done.5, bf16[1,8,128,128]{2,3,1,0:T(8,128)(2,1)S(1)} %fusion.98), kind=kOutput, calls=%fused_computation.62 | convolution fusion | flops 270532608 | bytes 8650752 | tf_op jit(solution)/shard_map/hse,hde->hsd/dot_general | solution.py:70
  294.9 3.9 %copy.17 = bf16[8,1024,128]{2,1,0:T(8,128)(2,1)} copy(bf16[8,1024,128]{1,2,0:T(8,128)(2,1)} %fusion.51) | data formatting | bytes 4194304
  (139 shorter events, 121.3 us)
Async XLA Ops:
  0.6 5.0 %copy-start.8 = (bf16[8,1024,128]{2,1,0:T(8,128)(2,1)S(1)}, bf16[8,1024,128]{2,1,0:T(8,128)(2,1)}, u32[]{:S(2)}) copy-start(bf16[8,1024,128]{2,1,0:T(8,128)(2,1)} %param.7) | copy-start | bytes 6291460
  5.6 2.4 copy-start.13
  9.6 6.5 %copy-start.11 = (f32[8,128,128]{2,1,0:T(8,128)}, f32[8,128,128]{2,1,0:T(8,128)S(1)}, u32[]{:S(2)}) copy-start(f32[8,128,128]{2,1,0:T(8,128)S(1)} %get-tuple-element.112) | copy-start | bytes 1572868
  10.3 5.8 %copy-start.9 = (f32[8,128,128]{2,1,0:T(8,128)}, f32[8,128,128]{2,1,0:T(8,128)S(1)}, u32[]{:S(2)}) copy-start(f32[8,128,128]{2,1,0:T(8,128)S(1)} %get-tuple-element.114) | copy-start | bytes 1572868
  11.1 5.0 %copy-start.12 = (f32[8,128,128]{2,1,0:T(8,128)}, f32[8,128,128]{2,1,0:T(8,128)S(1)}, u32[]{:S(2)}) copy-start(f32[8,128,128]{2,1,0:T(8,128)S(1)} %get-tuple-element.116) | copy-start | bytes 1572868
  11.1 5.0 %collective-permute-start.5 = (f32[5,8,128,128]{2,3,1,0:T(8,128)S(1)}, f32[5,8,128,128]{2,3,1,0:T(8,128)S(1)}, u32[]{:S(2)}, u32[]{:S(2)}) collective-permute-start(f32[5,8,128,128]{2,3,1,0:T(8,128)S(1)} %get-tuple-element.115), channel_id=1, source_target_pairs={{0,4},{4,0},{8,12},{12,8},{16,20},{20,16},{24,28},{28,24},{32,36},... | collective-permute-start | bytes 7864328 | tf_op jit(solution)/shard_map/ppermute | solution.py:8
  16.1 66.9 %copy-start.6 = (f32[5,8,128,128]{2,3,1,0:T(8,128)}, f32[5,8,128,128]{2,3,1,0:T(8,128)S(1)}, u32[]{:S(2)}) copy-start(f32[5,8,128,128]{2,3,1,0:T(8,128)S(1)} %collective-permute-done.5) | copy-start | bytes 7864324
  16.4 3.5 %copy-start.2 = (bf16[8,1024,128]{2,1,0:T(8,128)(2,1)S(1)}, bf16[8,1024,128]{2,1,0:T(8,128)(2,1)}, u32[]{:S(2)}) copy-start(bf16[8,1024,128]{2,1,0:T(8,128)(2,1)} %param.8) | copy-start | bytes 6291460
  16.4 3.6 %copy-start.4 = (bf16[8,1024,128]{2,1,0:T(8,128)(2,1)S(1)}, bf16[8,1024,128]{2,1,0:T(8,128)(2,1)}, u32[]{:S(2)}) copy-start(bf16[8,1024,128]{2,1,0:T(8,128)(2,1)} %param.9) | copy-start | bytes 6291460
  17.9 65.1 %collective-permute-start.6 = (f32[4,8,128,128]{2,3,1,0:T(8,128)}, f32[4,8,128,128]{2,3,1,0:T(8,128)}, u32[]{:S(2)}, u32[]{:S(2)}) collective-permute-start(f32[4,8,128,128]{2,3,1,0:T(8,128)} %pad_maximum_fusion), channel_id=1, source_target_pairs={{0,8},{4,12},{8,0},{12,4},{16,24},{20,28},{24,16},{28,20},{32,40},... | collective-permute-start | bytes 6291464 | tf_op jit(solution)/shard_map/ppermute | solution.py:8
  20.7 2.0 collective-permute-start
  23.5 53.8 %collective-permute-start.1 = (f32[8,128,128]{2,1,0:T(8,128)S(1)}, f32[8,128,128]{2,1,0:T(8,128)}, u32[]{:S(2)}, u32[]{:S(2)}) collective-permute-start(f32[8,128,128]{2,1,0:T(8,128)S(1)} %add.109), channel_id=1, source_target_pairs={{0,8},{4,12},{8,0},{12,4},{16,24},{20,28},{24,16},{28,20},{32,40},... | collective-permute-start | bytes 1572872 | tf_op jit(solution)/shard_map/ppermute | solution.py:8
  79.2 120.0 %collective-permute-start.2 = (f32[8,128,128]{2,1,0:T(8,128)}, f32[8,128,128]{2,1,0:T(8,128)}, u32[]{:S(2)}, u32[]{:S(2)}) collective-permute-start(f32[8,128,128]{2,1,0:T(8,128)} %add.112), channel_id=1, source_target_pairs={{0,16},{4,20},{8,24},{12,28},{16,0},{20,4},{24,8},{28,12},{32,48},... | collective-permute-start | bytes 1572872 | tf_op jit(solution)/shard_map/ppermute | solution.py:8
  86.4 116.0 %collective-permute-start.7 = (f32[3,8,128,128]{2,3,1,0:T(8,128)}, f32[3,8,128,128]{2,3,1,0:T(8,128)}, u32[]{:S(2)}, u32[]{:S(2)}) collective-permute-start(f32[3,8,128,128]{2,3,1,0:T(8,128)} %pad_maximum_fusion.1), channel_id=1, source_target_pairs={{0,16},{4,20},{8,24},{12,28},{16,0},{20,4},{24,8},{28,12},{32,48},... | collective-permute-start | bytes 4718600 | tf_op jit(solution)/shard_map/ppermute | solution.py:8
  197.4 4.9 %copy-start.10 = (f32[8,128,128]{2,1,0:T(8,128)S(1)}, f32[8,128,128]{2,1,0:T(8,128)}, u32[]{:S(2)}) copy-start(f32[8,128,128]{2,1,0:T(8,128)} %copy-done.9) | copy-start | bytes 1572868
  200.5 15.1 %collective-permute-start.3 = (f32[8,128,128]{2,1,0:T(8,128)S(1)}, f32[8,128,128]{2,1,0:T(8,128)S(1)}, u32[]{:S(2)}, u32[]{:S(2)}) collective-permute-start(f32[8,128,128]{2,1,0:T(8,128)S(1)} %add.115), channel_id=1, source_target_pairs={{0,32},{4,36},{8,40},{12,44},{16,48},{20,52},{24,56},{28,60},{32,0... | collective-permute-start | bytes 1572872 | tf_op jit(solution)/shard_map/ppermute | solution.py:8
  204.1 33.9 %collective-permute-start.8 = (f32[2,8,128,128]{2,3,1,0:T(8,128)S(1)}, f32[2,8,128,128]{2,3,1,0:T(8,128)S(1)}, u32[]{:S(2)}, u32[]{:S(2)}) collective-permute-start(f32[2,8,128,128]{2,3,1,0:T(8,128)S(1)} %pad_maximum_fusion.2), channel_id=1, source_target_pairs={{0,32},{4,36},{8,40},{12,44},{16,48},{20,52},{24,56},{28,60},{32,0... | collective-permute-start | bytes 3145736 | tf_op jit(solution)/shard_map/ppermute | solution.py:8
  215.6 36.1 %collective-permute-start.4 = (f32[8,128,128]{2,1,0:T(8,128)S(1)}, f32[8,128,128]{2,1,0:T(8,128)S(1)}, u32[]{:S(2)}, u32[]{:S(2)}) collective-permute-start(f32[8,128,128]{2,1,0:T(8,128)S(1)} %add.118), channel_id=1, source_target_pairs={{0,64},{4,68},{8,72},{12,76},{16,80},{20,84},{24,88},{28,92},{32,9... | collective-permute-start | bytes 1572872 | tf_op jit(solution)/shard_map/ppermute | solution.py:8
  221.5 30.2 %copy-start.7 = (bf16[8,1024,128]{1,2,0:T(8,128)(2,1)S(1)}, bf16[8,1024,128]{1,2,0:T(8,128)(2,1)}, u32[]{:S(2)}) copy-start(bf16[8,1024,128]{1,2,0:T(8,128)(2,1)} %copy.15) | copy-start | bytes 6291460
  238.0 2.3 copy-start.15
  240.3 40.3 %collective-permute-start.9 = (f32[1,8,128,128]{2,3,1,0:T(8,128)}, f32[1,8,128,128]{2,3,1,0:T(8,128)}, u32[]{:S(2)}, u32[]{:S(2)}) collective-permute-start(f32[1,8,128,128]{2,3,1,0:T(8,128)} %fusion.95), channel_id=1, source_target_pairs={{0,64},{4,68},{8,72},{12,76},{16,80},{20,84},{24,88},{28,92},{32,9... | collective-permute-start | bytes 1572872 | tf_op jit(solution)/shard_map/ppermute | solution.py:8
  258.8 21.8 %copy-start.16 = (f32[2,8,128,128]{2,3,1,0:T(8,128)S(1)}, f32[2,8,128,128]{2,3,1,0:T(8,128)}, u32[]{:S(2)}) copy-start(f32[2,8,128,128]{2,3,1,0:T(8,128)} %copy-done.15) | copy-start | bytes 3145732
  258.8 23.5 %copy-start.3 = (bf16[8,1024,128]{2,1,0:T(8,128)(2,1)S(1)}, bf16[8,1024,128]{2,1,0:T(8,128)(2,1)}, u32[]{:S(2)}) copy-start(bf16[8,1024,128]{2,1,0:T(8,128)(2,1)} %get-tuple-element.219) | copy-start | bytes 6291460
  286.6 4.1 %copy-start.5 = (bf16[8,1024,128]{2,1,0:T(8,128)(2,1)S(1)}, bf16[8,1024,128]{2,1,0:T(8,128)(2,1)}, u32[]{:S(2)}) copy-start(bf16[8,1024,128]{2,1,0:T(8,128)(2,1)} %get-tuple-element.220) | copy-start | bytes 6291460
  (10 other events, 18.4 us)
where the time goes:
time: 301 us; the launch traced here: 299 us
  matrix products  129 us (43%)
  waiting for transfers between devices  90.5 us (30%)
  local copies, waits for them, and re-layouts  29.6 us (10%)
  blocking collectives  17.7 us (6%)
  starting transfers between devices  16.9 us (6%)
  other arithmetic  14.2 us (5%)
    ppermute x10, waiting for transfers between devices, partner_2(): lax.ppermute(shard, axis, [(i, i ^ 1 << distance) for i in range(lax.axis...  90.5 us
    dot_general x8, matrix products, local_block(): jnp.einsum('ts,td->sd', attn, out_grad, preferred_element_type=jnp.float32)  30.7 us
    unnamed x37, local copies, waits for them, and re-layouts  21.6 us
    dot_general x8, matrix products, local_block(): jnp.einsum('ts,td->sd', d_raw, queries, preferred_element_type=jnp.float32)  20.8 us
    dot_general x8, matrix products, local_block(): jnp.einsum('ts,sd->td', d_raw, key_rows, preferred_element_type=jnp.float32)  18.6 us
    psum x1, blocking collectives, per_device(): weight_grad = lax.psum(jnp.stack(weight_rows, axis=0), 'head')  17.7 us
    ppermute x10, starting transfers between devices, partner_2(): lax.ppermute(shard, axis, [(i, i ^ 1 << distance) for i in range(lax.axis...  16.9 us
    dot_general x5, matrix products, per_device(): jnp.einsum('hte,hde->htd', out_grad, state_bf, preferred_element_type=jnp...  15 us
  transfers between devices with their start and end apart: 10, of which 6 were waited for; matrix products, arithmetic and copies ran while one was open for 47% of the time, Pallas kernels for 0%

commit v1 on v0

v1 whole, which is shorter than its diff:
```python
import functools

import jax
import jax.numpy as jnp
from jax import lax
from jax.experimental import pallas as pl
from jax.experimental.pallas import tpu as pltpu
from jax.sharding import PartitionSpec as P

F32, BF16 = jnp.float32, jnp.bfloat16
CHUNK = 256


def mm(a, b, ca, cb):
    return lax.dot_general(a, b, (((ca,), (cb,)), ((), ())), preferred_element_type=F32)


def spread_weights(w_ref, wb_ref):
    rows, length = w_ref.shape
    padded = jnp.concatenate([w_ref[...], w_ref[0 : 8 - rows, :]], axis=0)
    columns = padded.T
    for row in range(rows):
        wb_ref[row] = jnp.broadcast_to(columns[:, row : row + 1], (length, 128))


def first_kernel(q_ref, k_ref, v_ref, g_ref, w_ref, gs_ref, sg_ref, wb_ref):
    @pl.when(pl.program_id(0) == 0)
    def _():
        spread_weights(w_ref, wb_ref)

    gs_ref[0] = mm(k_ref[0], v_ref[0], 0, 0)
    levels = sg_ref.shape[0]
    g_f = g_ref[0].astype(F32)
    q_t = q_ref[0].T
    for level in range(levels):
        weighted = (wb_ref[1 + level] * g_f).astype(BF16)
        sg_ref[level, 0] = mm(q_t, weighted, 1, 0)


def last_kernel(q_ref, k_ref, v_ref, g_ref, w_ref, st_ref, gg_ref, qg_ref, kg_ref, vg_ref, wg_ref, wb_ref, acc_ref):
    head = pl.program_id(0)
    levels = st_ref.shape[0]
    length, dim = q_ref.shape[1:]
    chunks = length // CHUNK

    @pl.when(head == 0)
    def _():
        spread_weights(w_ref, wb_ref)
        acc_ref[...] = jnp.zeros_like(acc_ref)

    row = lax.broadcasted_iota(jnp.int32, (CHUNK, CHUNK), 0)
    col = lax.broadcasted_iota(jnp.int32, (CHUNK, CHUNK), 1)
    lower, upper = row >= col, row <= col
    parts = [pl.ds(c * CHUNK, CHUNK) for c in range(chunks)]
    suffix = [gg_ref[0].astype(F32)]
    for c in range(chunks - 1, 0, -1):
        g_0 = (wb_ref[0, parts[c]] * g_ref[0, parts[c]].astype(F32)).astype(BF16)
        suffix.append(suffix[-1] + mm(q_ref[0, parts[c]], g_0, 0, 0))
    suffix = [s.astype(BF16) for s in suffix[::-1]]
    prefix = jnp.zeros((dim, dim), F32)
    states = jnp.concatenate([st_ref[level, 0] for level in range(levels)], axis=0)
    for c in range(chunks):
        rows = parts[c]
        q, k, v, g = (ref[0, rows] for ref in (q_ref, k_ref, v_ref, g_ref))
        w_0 = wb_ref[0, rows]
        q_f = q.astype(F32)
        q_0 = (w_0 * q_f).astype(BF16)
        g_0 = (w_0 * g.astype(F32)).astype(BF16)
        raw_t = jnp.where(upper, mm(k, q, 1, 1), 0.0).astype(BF16)
        vg_ref[0, rows] = (mm(raw_t, g_0, 1, 0) + mm(k, suffix[c], 1, 0)).astype(BF16)
        da_t = jnp.where(upper, mm(v, g, 1, 1), 0.0).astype(BF16)
        kg_ref[0, rows] = (mm(da_t, q_0, 1, 0) + mm(v, suffix[c], 1, 1)).astype(BF16)
        da = jnp.where(lower, mm(g, v, 1, 1), 0.0).astype(BF16)
        z = mm(da, k, 1, 0)
        if c:
            z = z + mm(g, prefix.astype(BF16), 1, 1)
        total = w_0 * z
        acc_ref[0, rows] += q_f * z
        for level in range(levels):
            z = mm(g, states[level * dim : (level + 1) * dim], 1, 1)
            total = total + wb_ref[1 + level, rows] * z
            acc_ref[1 + level, rows] += q_f * z
        qg_ref[0, rows] = total.astype(BF16)
        if c < chunks - 1:
            prefix = prefix + mm(k, v, 0, 0)

    @pl.when(head == pl.num_programs(0) - 1)
    def _():
        ones = jnp.ones((8, dim), BF16)
        for level in range(levels + 1):
            term = acc_ref[level]
            high = term.astype(BF16)
            low = (term - high.astype(F32)).astype(BF16)
            sums = mm(ones, high, 1, 1) + mm(ones, low, 1, 1)
            wg_ref[level : level + 1, :] = sums[0:1]


def first_call(q, k, v, g, w, levels):
    heads, length, dim = q.shape
    block = pl.BlockSpec((1, length, dim), lambda h: (h, 0, 0))
    return pl.pallas_call(
        first_kernel,
        grid=(heads,),
        in_specs=[block] * 4 + [pl.BlockSpec(w.shape, lambda h: (0, 0))],
        out_specs=[
            pl.BlockSpec((1, dim, dim), lambda h: (h, 0, 0)),
            pl.BlockSpec((levels, 1, dim, dim), lambda h: (0, h, 0, 0)),
        ],
        out_shape=[
            jax.ShapeDtypeStruct((heads, dim, dim), F32),
            jax.ShapeDtypeStruct((levels, heads, dim, dim), F32),
        ],
        scratch_shapes=[pltpu.VMEM((levels + 1, length, dim), F32)],
        cost_estimate=pl.CostEstimate(flops=2 * 6 * q.size * dim, bytes_accessed=12 << 20, transcendentals=0),
    )(q, k, v, g, w)


def last_call(q, k, v, g, w, states, grad_bf):
    heads, length, dim = q.shape
    levels = states.shape[0]
    block = pl.BlockSpec((1, length, dim), lambda h: (h, 0, 0))
    whole = pl.BlockSpec(w.shape, lambda h: (0, 0))
    return pl.pallas_call(
        last_kernel,
        grid=(heads,),
        in_specs=[block] * 4
        + [
            whole,
            pl.BlockSpec((levels, 1, dim, dim), lambda h: (0, h, 0, 0)),
            pl.BlockSpec((1, dim, dim), lambda h: (h, 0, 0)),
        ],
        out_specs=[block] * 3 + [whole],
        out_shape=[jax.ShapeDtypeStruct(q.shape, BF16)] * 3 + [jax.ShapeDtypeStruct(w.shape, F32)],
        scratch_shapes=[pltpu.VMEM((levels + 1, length, dim), F32)] * 2,
        cost_estimate=pl.CostEstimate(flops=20 * q.size * dim, bytes_accessed=16 << 20, transcendentals=0),
    )(q, k, v, g, w, states, grad_bf)


def partner_2(shard, axis, distance):
    return lax.ppermute(shard, axis, [(i, i ^ 1 << distance) for i in range(lax.axis_size(axis))])


def per_device(queries, key_rows, value_rows, level_weight, out_grad):
    levels = lax.axis_size("ctx").bit_length() - 1
    position = lax.axis_index("ctx")
    bit_flags = [(position // 2**height % 2).astype(F32) for height in range(levels)]
    group_state, state_grad = first_call(queries, key_rows, value_rows, out_grad, level_weight, levels)
    running = group_state
    states = []
    adjoint = None
    for height in range(levels):
        partner = partner_2(running, "ctx", height)
        states.append(bit_flags[height] * partner)
        running = running + partner
        top = levels - 1 - height
        sent = bit_flags[top] * state_grad[top]
        if adjoint is not None:
            sent = sent + adjoint
        received = partner_2(sent, "ctx", top)
        adjoint = received if adjoint is None else adjoint + received
    query_grad, key_grad, value_grad, rows = last_call(
        queries, key_rows, value_rows, out_grad, level_weight,
        jnp.stack(states, axis=0).astype(BF16), adjoint.astype(BF16),
    )
    return query_grad, key_grad, value_grad, lax.psum(rows, "head")


def solution(mesh):
    rows = P("head", "ctx", None)
    return jax.shard_map(
        per_device,
        mesh=mesh,
        in_specs=(rows, rows, rows, P(None, "ctx"), rows),
        out_specs=(rows, rows, rows, P(None, "ctx")),
        check_vma=False,
    )
```

time: 301 us -> 145 us (0.48)
  matrix products: 129 us -> 0 us
  waiting for transfers between devices: 90.5 us -> 53.9 us
  Pallas kernels: 0 us -> 33.1 us
  local copies, waits for them, and re-layouts: 29.6 us -> 0.02 us
  other arithmetic: 14.2 us -> 20.4 us
    dot_general x53 -> x0, matrix products: 129 us -> none  [the longest x8 30.7 us: local_block(): jnp.einsum('ts,td->sd', attn, out_grad, preferred_element_type=jnp.float32)]
    ppermute x10, waiting for transfers between devices: 90.5 us -> 53.9 us  [partner_2(): lax.ppermute(shard, axis, [(i, i ^ 1 << distance) for i in range(lax.axis...]
    pallas_call x0 -> x2, Pallas kernels: none -> 33.1 us  [the longest x1 22.7 us: last_call(): pl.pallas_call(last_kernel, grid=(heads,), in_specs=[block] * 4 + [whole,...]
    unnamed x37 -> x10, local copies, waits for them, and re-layouts: 21.6 us -> 0.02 us
    another operation x10 -> x1, other arithmetic: 9.24 us -> 0.76 us  [per_device(): jnp.stack(states, axis=0).astype(BF16)]
    add x0 -> x4, other arithmetic: none -> 7.42 us  [per_device(): sent = sent + adjoint]
    slice x9 -> x0, local copies, waits for them, and re-layouts: 7.06 us -> none  [the longest x8 6.08 us: per_device(): level_weight[0]]
    unnamed x0 -> x4, other arithmetic: none -> 5.13 us
  transfers between devices with their start and end apart: 10 -> 10, of which waited for: 6 -> 6; matrix products, arithmetic and copies ran while one was open for 47% -> 12% of each run, Pallas kernels for 0% -> 0%
where the time goes in v1:
time: 145 us; the launch traced here: 144 us
  waiting for transfers between devices  53.9 us (37%)
  Pallas kernels  33.1 us (23%)
  other arithmetic  20.4 us (14%)
  blocking collectives  18.3 us (13%)
  starting transfers between devices  17.7 us (12%)
    ppermute x10, waiting for transfers between devices, partner_2(): lax.ppermute(shard, axis, [(i, i ^ 1 << distance) for i in range(lax.axis...  53.9 us
    pallas_call x1, Pallas kernels, last_call(): pl.pallas_call(last_kernel, grid=(heads,), in_specs=[block] * 4 + [whole,...  22.7 us
    psum x1, blocking collectives, per_device(): return (query_grad, key_grad, value_grad, lax.psum(rows, 'head'))  18.3 us
    ppermute x10, starting transfers between devices, partner_2(): lax.ppermute(shard, axis, [(i, i ^ 1 << distance) for i in range(lax.axis...  17.7 us
    pallas_call x1, Pallas kernels, first_call(): pl.pallas_call(first_kernel, grid=(heads,), in_specs=[block] * 4 + [pl.Bl...  10.4 us
    add x4, other arithmetic, per_device(): sent = sent + adjoint  7.42 us
    unnamed x4, other arithmetic  5.13 us
    add x4, other arithmetic, per_device(): running = running + partner  4.42 us
  transfers between devices with their start and end apart: 10, of which 6 were waited for; matrix products, arithmetic and copies ran while one was open for 12% of the time, Pallas kernels for 0%

profile of v1, /device:TPU:0, one launch (start us, length us, event | category | flops | bytes accessed | tf_op | source)
XLA Modules:
  0.0 144.1 jit_solution(6069066644680378595)
XLA Ops:
  0.7 10.4 %shard_map.84 = (f32[8,128,128]{2,1,0:T(8,128)}, f32[5,8,128,128]{3,2,1,0:T(8,128)}) custom-call(bf16[8,1024,128]{2,1,0:T(8,128)(2,1)} %q_ref.3, bf16[8,1024,128]{2,1,0:T(8,128)(2,1)} %k_ref.3, bf16[8,1024,128]{2,1,0:T(8,128)(2,1)} %v_ref.3, bf16[8,1024,128]{2,1,0:T(8,128)(2,1)} %g_ref.3, f32[6,1024]{1,0:T(8,128)} %w_ref.3), custom_call_target="tpu_custom_call" | custom-call | flops 1610612736 | bytes 12582912 | tf_op jit(solution)/shard_map/pallas_call | solution.py:101
  11.0 1.9 %multiply_bitcast_fusion = f32[8,128,128]{2,1,0:T(8,128)} fusion(f32[5,8,128,128]{3,2,1,0:T(8,128)} %get-tuple-element.11, f32[]{:T(128)S(6)} %convert_element_type.23), kind=kLoop, calls=%fused_computation.5 | loop fusion | flops 131072 | bytes 1048580 | tf_op jit(solution)/shard_map/mul | solution.py:156
  12.9 3.3 %collective-permute-start.5 = (f32[8,128,128]{2,1,0:T(8,128)}, f32[8,128,128]{2,1,0:T(8,128)S(1)}, u32[]{:S(2)}, u32[]{:S(2)}) collective-permute-start(f32[8,128,128]{2,1,0:T(8,128)} %multiply_bitcast_fusion), channel_id=1, source_target_pairs={{0,64},{4,68},{8,72},{12,76},{16,80},{20,84},{24,88},{28,92},{32,9... | collective-permute-start | bytes 1572872 | tf_op jit(solution)/shard_map/ppermute | solution.py:140
  16.2 12.1 %collective-permute-done.5 = f32[8,128,128]{2,1,0:T(8,128)S(1)} collective-permute-done((f32[8,128,128]{2,1,0:T(8,128)}, f32[8,128,128]{2,1,0:T(8,128)S(1)}, u32[]{:S(2)}, u32[]{:S(2)}) %collective-permute-start.5) | collective-permute-done | bytes 524320 | tf_op jit(solution)/shard_map/ppermute | solution.py:140
  28.4 2.1 %bitcast_add_fusion.3 = f32[8,128,128]{2,1,0:T(8,128)} fusion(f32[8,128,128]{2,1,0:T(8,128)S(1)} %collective-permute-done.5, f32[5,8,128,128]{3,2,1,0:T(8,128)} %get-tuple-element.11, f32[]{:T(128)S(6)} %convert_element_type.22), kind=kLoop, calls=%fused_computation.3 | loop fusion | flops 262144 | bytes 1572868 | tf_op jit(solution)/shard_map/add | solution.py:158
  30.4 1.6 %collective-permute-start.6 = (f32[8,128,128]{2,1,0:T(8,128)}, f32[8,128,128]{2,1,0:T(8,128)}, u32[]{:S(2)}, u32[]{:S(2)}) collective-permute-start(f32[8,128,128]{2,1,0:T(8,128)} %bitcast_add_fusion.3), channel_id=1, source_target_pairs={{0,32},{4,36},{8,40},{12,44},{16,48},{20,52},{24,56},{28,60},{32,0... | collective-permute-start | bytes 1572872 | tf_op jit(solution)/shard_map/ppermute | solution.py:140
  32.1 1.3 add.61
  33.4 2.0 %collective-permute-start.1 = (f32[8,128,128]{2,1,0:T(8,128)S(1)}, f32[8,128,128]{2,1,0:T(8,128)}, u32[]{:S(2)}, u32[]{:S(2)}) collective-permute-start(f32[8,128,128]{2,1,0:T(8,128)S(1)} %add.61), channel_id=1, source_target_pairs={{0,8},{4,12},{8,0},{12,4},{16,24},{20,28},{24,16},{28,20},{32,40},... | collective-permute-start | bytes 1572872 | tf_op jit(solution)/shard_map/ppermute | solution.py:140
  35.4 8.2 %collective-permute-done.6 = f32[8,128,128]{2,1,0:T(8,128)} collective-permute-done((f32[8,128,128]{2,1,0:T(8,128)}, f32[8,128,128]{2,1,0:T(8,128)}, u32[]{:S(2)}, u32[]{:S(2)}) %collective-permute-start.6) | collective-permute-done | bytes 524320 | tf_op jit(solution)/shard_map/ppermute | solution.py:140
  43.6 2.1 %bitcast_add_fusion.2 = (f32[8,128,128]{2,1,0:T(8,128)}, f32[8,128,128]{2,1,0:T(8,128)}) fusion(f32[5,8,128,128]{3,2,1,0:T(8,128)S(1)} %copy-done, f32[]{:T(128)S(6)} %convert_element_type.21, f32[8,128,128]{2,1,0:T(8,128)S(1)} %copy-done.2, f32[8,128,128]{2,1,0:T(8,128)} %collective-permute-done.6), kind=kLoop, calls=%fused_computation.2 | loop fusion | flops 393216 | bytes 2621444 | tf_op jit(solution)/shard_map/add | solution.py:158
  45.7 3.9 %collective-permute-start.7 = (f32[8,128,128]{2,1,0:T(8,128)}, f32[8,128,128]{2,1,0:T(8,128)}, u32[]{:S(2)}, u32[]{:S(2)}) collective-permute-start(f32[8,128,128]{2,1,0:T(8,128)} %get-tuple-element.20), channel_id=1, source_target_pairs={{0,16},{4,20},{8,24},{12,28},{16,0},{20,4},{24,8},{28,12},{32,48},... | collective-permute-start | bytes 1572872 | tf_op jit(solution)/shard_map/ppermute | solution.py:140
  49.6 1.9 %add.63 = f32[8,128,128]{2,1,0:T(8,128)} add(f32[8,128,128]{2,1,0:T(8,128)S(1)} %add.61, f32[8,128,128]{2,1,0:T(8,128)} %collective-permute-done.1) | non-fusion elementwise | flops 131072 | bytes 1572864 | tf_op jit(solution)/shard_map/add | solution.py:154
  51.9 10.8 %collective-permute-done.7 = f32[8,128,128]{2,1,0:T(8,128)} collective-permute-done((f32[8,128,128]{2,1,0:T(8,128)}, f32[8,128,128]{2,1,0:T(8,128)}, u32[]{:S(2)}, u32[]{:S(2)}) %collective-permute-start.7) | collective-permute-done | bytes 524320 | tf_op jit(solution)/shard_map/ppermute | solution.py:140
  62.7 2.1 %bitcast_add_fusion.1 = (f32[8,128,128]{2,1,0:T(8,128)}, f32[8,128,128]{2,1,0:T(8,128)}) fusion(f32[5,8,128,128]{3,2,1,0:T(8,128)S(1)} %copy-done, f32[]{:T(128)S(6)} %convert_element_type.20, f32[8,128,128]{2,1,0:T(8,128)S(1)} %copy-done.3, f32[8,128,128]{2,1,0:T(8,128)} %collective-permute-done.7), kind=kLoop, calls=%fused_computation.1 | loop fusion | flops 393216 | bytes 2621444 | tf_op jit(solution)/shard_map/add | solution.py:158
  64.8 1.6 %collective-permute-start.8 = (f32[8,128,128]{2,1,0:T(8,128)}, f32[8,128,128]{2,1,0:T(8,128)}, u32[]{:S(2)}, u32[]{:S(2)}) collective-permute-start(f32[8,128,128]{2,1,0:T(8,128)} %get-tuple-element.18), channel_id=1, source_target_pairs={{0,8},{4,12},{8,0},{12,4},{16,24},{20,28},{24,16},{28,20},{32,40},... | collective-permute-start | bytes 1572872 | tf_op jit(solution)/shard_map/ppermute | solution.py:140
  66.4 1.8 %fusion.1 = bf16[5,8,128,128]{3,2,1,0:T(8,128)(2,1)} fusion(f32[8,128,128]{2,1,0:T(8,128)} %collective-permute-done, f32[]{:T(128)S(6)} %convert_element_type.19), kind=kLoop, calls=%fused_computation.12 | loop fusion | flops 262143 | bytes 786436
  68.2 5.6 %collective-permute-done.2 = f32[8,128,128]{2,1,0:T(8,128)S(1)} collective-permute-done((f32[8,128,128]{2,1,0:T(8,128)}, f32[8,128,128]{2,1,0:T(8,128)S(1)}, u32[]{:S(2)}, u32[]{:S(2)}) %collective-permute-start.2) | collective-permute-done | bytes 524320 | tf_op jit(solution)/shard_map/ppermute | solution.py:140
  74.9 1.7 %collective-permute-start.3 = (f32[8,128,128]{2,1,0:T(8,128)S(1)}, f32[8,128,128]{2,1,0:T(8,128)S(1)}, u32[]{:S(2)}, u32[]{:S(2)}) collective-permute-start(f32[8,128,128]{2,1,0:T(8,128)S(1)} %add.65), channel_id=1, source_target_pairs={{0,32},{4,36},{8,40},{12,44},{16,48},{20,52},{24,56},{28,60},{32,0... | collective-permute-start | bytes 1572872 | tf_op jit(solution)/shard_map/ppermute | solution.py:140
  76.6 6.8 %collective-permute-done.8 = f32[8,128,128]{2,1,0:T(8,128)} collective-permute-done((f32[8,128,128]{2,1,0:T(8,128)}, f32[8,128,128]{2,1,0:T(8,128)}, u32[]{:S(2)}, u32[]{:S(2)}) %collective-permute-start.8) | collective-permute-done | bytes 524320 | tf_op jit(solution)/shard_map/ppermute | solution.py:140
  84.6 1.8 %fusion.3 = bf16[5,8,128,128]{3,2,1,0:T(8,128)(2,1)} fusion(bf16[5,8,128,128]{3,2,1,0:T(8,128)(2,1)} %fusion.1, f32[8,128,128]{2,1,0:T(8,128)} %collective-permute-done.1, f32[]{:T(128)S(6)} %convert_element_type.20), kind=kLoop, calls=%fused_computation.14 | loop fusion | flops 262144 | bytes 786436
  86.4 3.3 %collective-permute-start.4 = (f32[8,128,128]{2,1,0:T(8,128)S(1)}, f32[8,128,128]{2,1,0:T(8,128)S(1)}, u32[]{:S(2)}, u32[]{:S(2)}) collective-permute-start(f32[8,128,128]{2,1,0:T(8,128)S(1)} %add.67), channel_id=1, source_target_pairs={{0,64},{4,68},{8,72},{12,76},{16,80},{20,84},{24,88},{28,92},{32,9... | collective-permute-start | bytes 1572872 | tf_op jit(solution)/shard_map/ppermute | solution.py:140
  92.0 10.3 %collective-permute-done.4 = f32[8,128,128]{2,1,0:T(8,128)S(1)} collective-permute-done((f32[8,128,128]{2,1,0:T(8,128)S(1)}, f32[8,128,128]{2,1,0:T(8,128)S(1)}, u32[]{:S(2)}, u32[]{:S(2)}) %collective-permute-start.4) | collective-permute-done | bytes 524320 | tf_op jit(solution)/shard_map/ppermute | solution.py:140
  103.1 22.7 %shard_map.85 = (bf16[8,1024,128]{2,1,0:T(8,128)(2,1)}, bf16[8,1024,128]{2,1,0:T(8,128)(2,1)}, bf16[8,1024,128]{2,1,0:T(8,128)(2,1)}, f32[6,1024]{1,0:T(8,128)}) custom-call(bf16[8,1024,128]{2,1,0:T(8,128)(2,1)} %q_ref.3, bf16[8,1024,128]{2,1,0:T(8,128)(2,1)} %k_ref.3, bf16[8,1024,128]{2,1,0:T(8,128)(2,1)} %v_ref.3, bf16[8,1024,128]{2,1,0:T(8,128)(2,1)} %g_ref.3, ...), custom_call_target="tpu_custom_call" | custom-call | flops 2684354560 | bytes 16777216 | tf_op jit(solution)/shard_map/pallas_call | solution.py:123
  125.8 18.3 %psum.7 = f32[6,1024]{1,0:T(8,128)} all-reduce(f32[6,1024]{1,0:T(8,128)} %get-tuple-element.15), channel_id=1, replica_groups=mesh['ctx'=32,'head'=4] {'head'}, use_global_device_ids=true, to_apply=%region_0.1 | all-reduce | flops 6144 | bytes 49152 | tf_op jit(solution)/shard_map/psum | solution.py:165
  (24 shorter events, 5.8 us)
Async XLA Ops:
  12.9 15.4 %collective-permute-start.5 = (f32[8,128,128]{2,1,0:T(8,128)}, f32[8,128,128]{2,1,0:T(8,128)S(1)}, u32[]{:S(2)}, u32[]{:S(2)}) collective-permute-start(f32[8,128,128]{2,1,0:T(8,128)} %multiply_bitcast_fusion), channel_id=1, source_target_pairs={{0,64},{4,68},{8,72},{12,76},{16,80},{20,84},{24,88},{28,92},{32,9... | collective-permute-start | bytes 1572872 | tf_op jit(solution)/shard_map/ppermute | solution.py:140
  16.2 15.8 %collective-permute-start = (f32[8,128,128]{2,1,0:T(8,128)}, f32[8,128,128]{2,1,0:T(8,128)}, u32[]{:S(2)}, u32[]{:S(2)}) collective-permute-start(f32[8,128,128]{2,1,0:T(8,128)} %get-tuple-element.10), channel_id=1, source_target_pairs={{0,4},{4,0},{8,12},{12,8},{16,20},{20,16},{24,28},{28,24},{32,36},... | collective-permute-start | bytes 1572872 | tf_op jit(solution)/shard_map/ppermute | solution.py:140
  16.2 27.4 %copy-start = (f32[5,8,128,128]{3,2,1,0:T(8,128)S(1)}, f32[5,8,128,128]{3,2,1,0:T(8,128)}, u32[]{:S(2)}) copy-start(f32[5,8,128,128]{3,2,1,0:T(8,128)} %get-tuple-element.11) | copy-start | bytes 7864324
  28.4 3.7 %copy-start.1 = (f32[8,128,128]{2,1,0:T(8,128)}, f32[8,128,128]{2,1,0:T(8,128)S(1)}, u32[]{:S(2)}) copy-start(f32[8,128,128]{2,1,0:T(8,128)S(1)} %collective-permute-done.5) | copy-start | bytes 1572868
  30.4 13.2 %collective-permute-start.6 = (f32[8,128,128]{2,1,0:T(8,128)}, f32[8,128,128]{2,1,0:T(8,128)}, u32[]{:S(2)}, u32[]{:S(2)}) collective-permute-start(f32[8,128,128]{2,1,0:T(8,128)} %bitcast_add_fusion.3), channel_id=1, source_target_pairs={{0,32},{4,36},{8,40},{12,44},{16,48},{20,52},{24,56},{28,60},{32,0... | collective-permute-start | bytes 1572872 | tf_op jit(solution)/shard_map/ppermute | solution.py:140
  32.1 11.5 %copy-start.2 = (f32[8,128,128]{2,1,0:T(8,128)S(1)}, f32[8,128,128]{2,1,0:T(8,128)}, u32[]{:S(2)}) copy-start(f32[8,128,128]{2,1,0:T(8,128)} %copy-done.1) | copy-start | bytes 1572868
  33.4 16.2 %collective-permute-start.1 = (f32[8,128,128]{2,1,0:T(8,128)S(1)}, f32[8,128,128]{2,1,0:T(8,128)}, u32[]{:S(2)}, u32[]{:S(2)}) collective-permute-start(f32[8,128,128]{2,1,0:T(8,128)S(1)} %add.61), channel_id=1, source_target_pairs={{0,8},{4,12},{8,0},{12,4},{16,24},{20,28},{24,16},{28,20},{32,40},... | collective-permute-start | bytes 1572872 | tf_op jit(solution)/shard_map/ppermute | solution.py:140
  45.7 17.0 %collective-permute-start.7 = (f32[8,128,128]{2,1,0:T(8,128)}, f32[8,128,128]{2,1,0:T(8,128)}, u32[]{:S(2)}, u32[]{:S(2)}) collective-permute-start(f32[8,128,128]{2,1,0:T(8,128)} %get-tuple-element.20), channel_id=1, source_target_pairs={{0,16},{4,20},{8,24},{12,28},{16,0},{20,4},{24,8},{28,12},{32,48},... | collective-permute-start | bytes 1572872 | tf_op jit(solution)/shard_map/ppermute | solution.py:140
  49.6 13.1 %copy-start.3 = (f32[8,128,128]{2,1,0:T(8,128)S(1)}, f32[8,128,128]{2,1,0:T(8,128)}, u32[]{:S(2)}) copy-start(f32[8,128,128]{2,1,0:T(8,128)} %get-tuple-element.21) | copy-start | bytes 1572868
  51.6 22.3 %collective-permute-start.2 = (f32[8,128,128]{2,1,0:T(8,128)}, f32[8,128,128]{2,1,0:T(8,128)S(1)}, u32[]{:S(2)}, u32[]{:S(2)}) collective-permute-start(f32[8,128,128]{2,1,0:T(8,128)} %add.63), channel_id=1, source_target_pairs={{0,16},{4,20},{8,24},{12,28},{16,0},{20,4},{24,8},{28,12},{32,48},... | collective-permute-start | bytes 1572872 | tf_op jit(solution)/shard_map/ppermute | solution.py:140
  64.8 18.5 %collective-permute-start.8 = (f32[8,128,128]{2,1,0:T(8,128)}, f32[8,128,128]{2,1,0:T(8,128)}, u32[]{:S(2)}, u32[]{:S(2)}) collective-permute-start(f32[8,128,128]{2,1,0:T(8,128)} %get-tuple-element.18), channel_id=1, source_target_pairs={{0,8},{4,12},{8,0},{12,4},{16,24},{20,28},{24,16},{28,20},{32,40},... | collective-permute-start | bytes 1572872 | tf_op jit(solution)/shard_map/ppermute | solution.py:140
  66.4 17.0 %copy-start.4 = (f32[8,128,128]{2,1,0:T(8,128)S(1)}, f32[8,128,128]{2,1,0:T(8,128)}, u32[]{:S(2)}) copy-start(f32[8,128,128]{2,1,0:T(8,128)} %get-tuple-element.19) | copy-start | bytes 1572868
  74.9 11.4 %collective-permute-start.3 = (f32[8,128,128]{2,1,0:T(8,128)S(1)}, f32[8,128,128]{2,1,0:T(8,128)S(1)}, u32[]{:S(2)}, u32[]{:S(2)}) collective-permute-start(f32[8,128,128]{2,1,0:T(8,128)S(1)} %add.65), channel_id=1, source_target_pairs={{0,32},{4,36},{8,40},{12,44},{16,48},{20,52},{24,56},{28,60},{32,0... | collective-permute-start | bytes 1572872 | tf_op jit(solution)/shard_map/ppermute | solution.py:140
  84.5 6.7 %collective-permute-start.9 = (f32[8,128,128]{2,1,0:T(8,128)S(1)}, f32[8,128,128]{2,1,0:T(8,128)S(1)}, u32[]{:S(2)}, u32[]{:S(2)}) collective-permute-start(f32[8,128,128]{2,1,0:T(8,128)S(1)} %get-tuple-element.16), channel_id=1, source_target_pairs={{0,4},{4,0},{8,12},{12,8},{16,20},{20,16},{24,28},{28,24},{32,36},... | collective-permute-start | bytes 1572872 | tf_op jit(solution)/shard_map/ppermute | solution.py:140
  86.4 15.9 %collective-permute-start.4 = (f32[8,128,128]{2,1,0:T(8,128)S(1)}, f32[8,128,128]{2,1,0:T(8,128)S(1)}, u32[]{:S(2)}, u32[]{:S(2)}) collective-permute-start(f32[8,128,128]{2,1,0:T(8,128)S(1)} %add.67), channel_id=1, source_target_pairs={{0,64},{4,68},{8,72},{12,76},{16,80},{20,84},{24,88},{28,92},{32,9... | collective-permute-start | bytes 1572872 | tf_op jit(solution)/shard_map/ppermute | solution.py:140

commit v2 on v1

--- a/solution.py
+++ b/solution.py
@@ -136,33 +136,201 @@
     )(q, k, v, g, w, states, grad_bf)
 
 
-def partner_2(shard, axis, distance):
-    return lax.ppermute(shard, axis, [(i, i ^ 1 << distance) for i in range(lax.axis_size(axis))])
+MESH = pl.DeviceIdType.MESH
+
+
+class Wires:
+    def __init__(self, send_sem, recv_sem):
+        self.sems = (send_sem, recv_sem)
+        self.count = 0
+
+    def send(self, src, dst, device):
+        copy = pltpu.make_async_remote_copy(
+            src_ref=src, dst_ref=dst, send_sem=self.sems[0].at[self.count],
+            recv_sem=self.sems[1].at[self.count], device_id=device, device_id_type=MESH,
+        )
+        self.count += 1
+        copy.start()
+        return copy
+
+
+def greet(devices):
+    barrier = pltpu.get_barrier_semaphore()
+    for device in devices:
+        pl.semaphore_signal(barrier, inc=1, device_id=device, device_id_type=MESH)
+    pl.semaphore_wait(barrier, len(devices))
+
+
+def gather_start(wires, mine, got, low, high, lower, upper):
+    first = (wires.send(mine.at[high], got.at[0, high], upper), wires.send(mine.at[low], got.at[1, low], lower))
+    second = (wires.send(mine.at[low], got.at[0, low], upper), wires.send(mine.at[high], got.at[1, high], lower))
+    return first, second
+
+
+def gather_relay(wires, first, got, low, high, lower, upper):
+    first[0].wait_recv()
+    up = wires.send(got.at[0, high], got.at[2, high], upper)
+    first[1].wait_recv()
+    down = wires.send(got.at[1, low], got.at[2, low], lower)
+    return up, down
+
+
+def reduce_start(wires, message, relay, got, low, high, lower, upper):
+    first = (wires.send(message.at[2, low], relay.at[0], upper), wires.send(message.at[2, high], relay.at[1], lower))
+    second = (wires.send(message.at[0, high], got.at[0, high], upper), wires.send(message.at[1, low], got.at[1, low], lower))
+    return first, second
+
+
+def reduce_relay(wires, first, message, relay, got, low, high, lower, upper):
+    first[0].wait_recv()
+    message[0, low] = message[0, low] + relay[0]
+    up = wires.send(message.at[0, low], got.at[0, low], upper)
+    first[1].wait_recv()
+    message[1, high] = message[1, high] + relay[1]
+    down = wires.send(message.at[1, high], got.at[1, high], lower)
+    return up, down
+
+
+def exchange_kernel(gs_ref, sg_ref, st_out, gg_out, gs_in, sg_in, sg0_in, mine_z, mine_y, got_z, got_y,
+                    msg_y, msg_z, rel_y, rel_z, back_y, back_z, st, gg, send_sem, recv_sem):
+    wires = Wires(send_sem, recv_sem)
+    me = lax.axis_index("ctx")
+    core, z, y = me % 2, me // 2 % 4, me // 8
+    heads = gs_ref.shape[0]
+    half = heads // 2
+    own, other = pl.ds(half * core, half), pl.ds(half * (1 - core), half)
+    low, high = pl.ds(0, half // 2), pl.ds(half // 2, half // 2)
+
+    def at(y, z, core):
+        return {"ctx": ((y + 4) % 4 * 4 + (z + 4) % 4) * 2 + core}
+
+    def flag(condition):
+        return jnp.where(condition, 1.0, 0.0).astype(F32)
+
+    mate = at(y, z, 1 - core)
+    z_ends = (at(y, z - 1, core), at(y, z + 1, core))
+    y_ends = (at(y - 1, z, core), at(y + 1, z, core))
+    greet((mate, *z_ends, *y_ends))
+
+    d_34 = wires.send(sg_ref.at[pl.ds(3, 2), other], sg_in.at[pl.ds(2, 2)], mate)
+    d_gs = wires.send(gs_ref, gs_in, mate)
+    d_12 = wires.send(sg_ref.at[pl.ds(1, 2), other], sg_in.at[pl.ds(0, 2)], mate)
+    d_0 = wires.send(sg_ref.at[0], sg0_in, mate)
+
+    d_34.wait_recv()
+    sum_3 = sg_ref[3, own] + sg_in[2]
+    sum_4 = sg_ref[4, own] + sg_in[3]
+    msg_y[0] = flag(y == 3) * sum_4
+    msg_y[1] = flag(y % 2 == 1) * sum_3 + flag(y == 2) * sum_4
+    msg_y[2] = flag(y >= 2) * sum_4
+    b_1, b_2 = reduce_start(wires, msg_y, rel_y, back_y, low, high, *y_ends)
+
+    d_gs.wait_recv()
+    mine_z[...] = gs_ref[own] + gs_in[own]
+    f_1, f_2 = gather_start(wires, mine_z, got_z, low, high, *z_ends)
+    b_3 = reduce_relay(wires, b_1, msg_y, rel_y, back_y, low, high, *y_ends)
+    f_3 = gather_relay(wires, f_1, got_z, low, high, *z_ends)
+    st_out[0] = (flag(core == 1) * gs_in[...]).astype(BF16)
+    d_12.wait_recv()
+
+    for copy in (*b_2, *b_3):
+        copy.wait_recv()
+    adjoint = back_y[0] + back_y[1]
+    sum_1 = sg_ref[1, own] + sg_in[0]
+    sum_2 = sg_ref[2, own] + sg_in[1]
+    msg_z[0] = adjoint + flag(z == 3) * sum_2
+    msg_z[1] = adjoint + flag(z % 2 == 1) * sum_1 + flag(z == 2) * sum_2
+    msg_z[2] = adjoint + flag(z >= 2) * sum_2
+    c_1, c_2 = reduce_start(wires, msg_z, rel_z, back_z, low, high, *z_ends)
+
+    for copy in (*f_2, *f_3):
+        copy.wait_recv()
+    mine_y[...] = mine_z[...] + got_z[0] + got_z[1] + got_z[2]
+    g_1, g_2 = gather_start(wires, mine_y, got_y, low, high, *y_ends)
+    st[0, own] = flag(z % 2 == 1) * got_z[0]
+    st[1, own] = flag(z >= 2) * got_z[2] + flag(z == 2) * got_z[0] + flag(z == 3) * got_z[1]
+    t_1 = wires.send(st.at[pl.ds(0, 2), own], st.at[pl.ds(0, 2), own], mate)
+    c_3 = reduce_relay(wires, c_1, msg_z, rel_z, back_z, low, high, *z_ends)
+    g_3 = gather_relay(wires, g_1, got_y, low, high, *y_ends)
+
+    for copy in (*c_2, *c_3):
+        copy.wait_recv()
+    gg[own] = adjoint + back_z[0] + back_z[1]
+    t_2 = wires.send(gg.at[own], gg.at[own], mate)
+    for copy in (*g_2, *g_3):
+        copy.wait_recv()
+    st[2, own] = flag(y % 2 == 1) * got_y[0]
+    st[3, own] = flag(y >= 2) * got_y[2] + flag(y == 2) * got_y[0] + flag(y == 3) * got_y[1]
+    t_3 = wires.send(st.at[pl.ds(2, 2), own], st.at[pl.ds(2, 2), own], mate)
+    d_0.wait_recv()
+    t_2.wait_recv()
+    gg_out[...] = (gg[...] + flag(core == 0) * sg0_in[...]).astype(BF16)
+    t_1.wait_recv()
+    st_out[1:3] = st[0:2].astype(BF16)
+    t_3.wait_recv()
+    st_out[3:5] = st[2:4].astype(BF16)
+    for copy in (d_34, d_gs, d_12, d_0, *b_1, *b_2, *b_3, *f_1, *f_2, *f_3, *c_1, *c_2, *c_3, *g_1, *g_2, *g_3, t_1, t_2, t_3):
+        copy.wait_send()
+
+
+def exchange_call(group_state, state_grad):
+    levels, heads, dim, _ = state_grad.shape
+    half = heads // 2
+    vmem = pl.BlockSpec(memory_space=pltpu.VMEM)
+
+    def block(*lead):
+        return pltpu.VMEM((*lead, dim, dim), F32)
+
+    return pl.pallas_call(
+        exchange_kernel,
+        in_specs=[vmem] * 2,
+        out_specs=[vmem] * 2,
+        out_shape=[jax.ShapeDtypeStruct(state_grad.shape, BF16), jax.ShapeDtypeStruct(group_state.shape, BF16)],
+        scratch_shapes=[
+            block(heads), block(levels - 1, half), block(heads), block(half), block(half), block(3, half), block(3, half),
+            block(3, half), block(3, half), block(2, half // 2), block(2, half // 2), block(2, half), block(2, half),
+            block(levels - 1, heads), block(heads), pltpu.SemaphoreType.DMA((31,)), pltpu.SemaphoreType.DMA((31,)),
+        ],
+        compiler_params=pltpu.CompilerParams(collective_id=0, has_side_effects=True),
+    )(group_state, state_grad)
+
+
+def total_kernel(count, rows_ref, out_ref, slots, send_sem, recv_sem):
+    wires = Wires(send_sem, recv_sem)
+    me = lax.axis_index("head")
+    peers = [{"head": (me + step) % count} for step in range(1, count)]
+    greet(peers)
+    copies = [wires.send(rows_ref, slots.at[me], peer) for peer in peers]
+    slots[me] = rows_ref[...]
+    for copy in copies:
+        copy.wait_recv()
+    total = slots[0]
+    for index in range(1, count):
+        total = total + slots[index]
+    out_ref[...] = total
+    for copy in copies:
+        copy.wait_send()
+
+
+def total_call(rows, count):
+    vmem = pl.BlockSpec(memory_space=pltpu.VMEM)
+    return pl.pallas_call(
+        functools.partial(total_kernel, count),
+        in_specs=[vmem],
+        out_specs=vmem,
+        out_shape=jax.ShapeDtypeStruct(rows.shape, F32),
+        scratch_shapes=[pltpu.VMEM((count, *rows.shape), F32)] + [pltpu.SemaphoreType.DMA((count - 1,))] * 2,
+        compiler_params=pltpu.CompilerParams(collective_id=1, has_side_effects=True),
+    )(rows)
 
 
 def per_device(queries, key_rows, value_rows, level_weight, out_grad):
     levels = lax.axis_size("ctx").bit_length() - 1
-    position = lax.axis_index("ctx")
-    bit_flags = [(position // 2**height % 2).astype(F32) for height in range(levels)]
     group_state, state_grad = first_call(queries, key_rows, value_rows, out_grad, level_weight, levels)
-    running = group_state
-    states = []
-    adjoint = None
-    for height in range(levels):
-        partner = partner_2(running, "ctx", height)
-        states.append(bit_flags[height] * partner)
-        running = running + partner
-        top = levels - 1 - height
-        sent = bit_flags[top] * state_grad[top]
-        if adjoint is not None:
-            sent = sent + adjoint
-        received = partner_2(sent, "ctx", top)
-        adjoint = received if adjoint is None else adjoint + received
+    states, grad_bf = exchange_call(group_state, state_grad)
     query_grad, key_grad, value_grad, rows = last_call(
-        queries, key_rows, value_rows, out_grad, level_weight,
-        jnp.stack(states, axis=0).astype(BF16), adjoint.astype(BF16),
-    )
-    return query_grad, key_grad, value_grad, lax.psum(rows, "head")
+        queries, key_rows, value_rows, out_grad, level_weight, states, grad_bf)
+    return query_grad, key_grad, value_grad, total_call(rows, lax.axis_size("head"))
 
 
 def solution(mesh):

time: 145 us -> 78.6 us (0.54)
  waiting for transfers between devices: 53.9 us -> 0 us
  Pallas kernels: 33.1 us -> 75.9 us
  other arithmetic: 20.4 us -> 0 us
  blocking collectives: 18.3 us -> 0 us
  starting transfers between devices: 17.7 us -> 0 us
    ppermute x10 -> x0, waiting for transfers between devices: 53.9 us -> none  [partner_2(): lax.ppermute(shard, axis, [(i, i ^ 1 << distance) for i in range(lax.axis...]
    pallas_call x0 -> x2, Pallas kernels: none -> 42.8 us  [the longest x1 34.6 us: exchange_call(): pl.pallas_call(exchange_kernel, in_specs=[vmem] * 2, out_specs=[vmem] * 2...]
    psum x1 -> x0, blocking collectives: 18.3 us -> none  [per_device(): return (query_grad, key_grad, value_grad, lax.psum(rows, 'head'))]
    ppermute x10 -> x0, starting transfers between devices: 17.7 us -> none  [partner_2(): lax.ppermute(shard, axis, [(i, i ^ 1 << distance) for i in range(lax.axis...]
    add x8 -> x0, other arithmetic: 11.8 us -> none  [the longest x4 7.42 us: per_device(): sent = sent + adjoint]
    unnamed x4 -> x0, other arithmetic: 5.13 us -> none
    mul x1 -> x0, other arithmetic: 1.88 us -> none  [per_device(): sent = bit_flags[top] * state_grad[top]]
  transfers between devices with their start and end apart: 10 -> 0, of which waited for: 6 -> 0; matrix products, arithmetic and copies ran while one was open for 12% -> 0% of each run, Pallas kernels for 0% -> 0%
where the time goes in v2:
time: 78.6 us; the launch traced here: 77.9 us
  Pallas kernels  75.9 us (97%)
  local copies, waits for them, and re-layouts  1.38 us (2%)
    pallas_call x1, Pallas kernels, exchange_call(): pl.pallas_call(exchange_kernel, in_specs=[vmem] * 2, out_specs=[vmem] * 2...  34.6 us
    pallas_call x1, Pallas kernels, last_call(): pl.pallas_call(last_kernel, grid=(heads,), in_specs=[block] * 4 + [whole,...  22.8 us
    pallas_call x1, Pallas kernels, first_call(): pl.pallas_call(first_kernel, grid=(heads,), in_specs=[block] * 4 + [pl.Bl...  10.4 us
    pallas_call x1, Pallas kernels, total_call(): pl.pallas_call(functools.partial(total_kernel, count), in_specs=[vmem], o...  8.18 us

profile of v2, /device:TPU:0, one launch (start us, length us, event | category | flops | bytes accessed | tf_op | source)
XLA Modules:
  0.0 77.9 jit_solution(3133106400675231624)
XLA Ops:
  0.6 10.4 %shard_map.84 = (f32[8,128,128]{2,1,0:T(8,128)}, f32[5,8,128,128]{3,2,1,0:T(8,128)}) custom-call(bf16[8,1024,128]{2,1,0:T(8,128)(2,1)} %q_ref.3, bf16[8,1024,128]{2,1,0:T(8,128)(2,1)} %k_ref.3, bf16[8,1024,128]{2,1,0:T(8,128)(2,1)} %v_ref.3, bf16[8,1024,128]{2,1,0:T(8,128)(2,1)} %g_ref.3, f32[6,1024]{1,0:T(8,128)} %w_ref.3), custom_call_target="tpu_custom_call" | custom-call | flops 1610612736 | bytes 12582912 | tf_op jit(solution)/shard_map/pallas_call | solution.py:101
  11.0 34.6 %shard_map.85 = (bf16[5,8,128,128]{3,2,1,0:T(8,128)(2,1)}, bf16[8,128,128]{2,1,0:T(8,128)(2,1)}) custom-call(f32[8,128,128]{2,1,0:T(8,128)} %get-tuple-element.12.gs_ref, f32[5,8,128,128]{3,2,1,0:T(8,128)} %get-tuple-element.13.sg_ref), custom_call_target="tpu_custom_call" | custom-call | tf_op jit(solution)/shard_map/pallas_call | solution.py:284
  45.6 22.8 %shard_map.86 = (bf16[8,1024,128]{2,1,0:T(8,128)(2,1)}, bf16[8,1024,128]{2,1,0:T(8,128)(2,1)}, bf16[8,1024,128]{2,1,0:T(8,128)(2,1)}, f32[6,1024]{1,0:T(8,128)}) custom-call(bf16[8,1024,128]{2,1,0:T(8,128)(2,1)} %q_ref.3, bf16[8,1024,128]{2,1,0:T(8,128)(2,1)} %k_ref.3, bf16[8,1024,128]{2,1,0:T(8,128)(2,1)} %v_ref.3, bf16[8,1024,128]{2,1,0:T(8,128)(2,1)} %g_ref.3, ...), custom_call_target="tpu_custom_call" | custom-call | flops 2684354560 | bytes 16777216 | tf_op jit(solution)/shard_map/pallas_call | solution.py:123
  68.4 8.2 %shard_map.87 = f32[6,1024]{1,0:T(8,128)} custom-call(f32[6,1024]{1,0:T(8,128)} %get-tuple-element.19.rows_ref), custom_call_target="tpu_custom_call" | custom-call | tf_op jit(solution)/shard_map/pallas_call | solution.py:317
  76.6 1.4 %copy.10 = f32[6,1024]{1,0:T(8,128)} copy(f32[6,1024]{1,0:T(8,128)} %shard_map.87) | data formatting | bytes 49152

commit v3 on v0

v3 whole, which is shorter than its diff:
```python
import jax
import jax.numpy as jnp
from jax import lax
from jax.experimental import pallas as pl
from jax.experimental.pallas import tpu as pltpu
from jax.sharding import PartitionSpec as P

F32, BF16 = jnp.float32, jnp.bfloat16
MESH = pl.DeviceIdType.MESH
CHUNK = 256
ARRIVALS = (
    (0, 0), (0, 1), (0, 2), (1, 0), (0, 3), (1, 1), (1, 2), (2, 0),
    (1, 3), (2, 1), (2, 2), (3, 0), (2, 3), (3, 1), (3, 2), (3, 3),
)


def mm(a, b, ca, cb):
    return lax.dot_general(a, b, (((ca,), (cb,)), ((), ())), preferred_element_type=F32)


def whole_kernel(q_hbm, k_hbm, v_hbm, g_hbm, w_ref, qg_hbm, kg_hbm, vg_hbm, wg_ref,
                 q_ref, k_ref, v_ref, g_ref, qg_ref, kg_ref, vg_ref, tot, pk, pv, wb, acc,
                 loc, in_own, in_other, f_run, f_got, b_msg, b_got, adj, st0, st, gg, prefix, suffix, slots,
                 in_sem, out_sem, d_sem, f_sem, b_sem, s_sem, t_sem, w_sem):
    me, mine = lax.axis_index("ctx"), lax.axis_index("head")
    core, z, y = me % 2, me // 2 % 4, me // 8
    heads, length, dim = q_ref.shape
    half, chunks, levels = heads // 2, length // CHUNK, 5
    parts = [pl.ds(c * CHUNK, CHUNK) for c in range(chunks)]
    own, other = half * core, half * (1 - core)

    def at(y, z, core):
        return {"ctx": (y * 4 + z) * 2 + core}

    def flag(condition):
        return jnp.where(condition, 1.0, 0.0).astype(F32)

    mate = at(y, z, 1 - core)
    z_near, z_far = at(y, z + 1 - 2 * (z % 2), core), at(y, 3 - z, core)
    y_near, y_far = at(y + 1 - 2 * (y % 2), z, core), at(3 - y, z, core)
    f_peer = (z_near, z_far, y_near, y_far)
    b_peer = f_peer[::-1]
    bits = (flag(z % 2 == 1), flag(z >= 2), flag(y % 2 == 1), flag(y >= 2))
    head_count = 4
    head_peers = [{"head": (mine + step) % head_count} for step in range(1, head_count)]

    def remote(src, dst, sems, index, device):
        return pltpu.make_async_remote_copy(
            src_ref=src, dst_ref=dst, send_sem=sems.at[(0, *index)], recv_sem=sems.at[(1, *index)],
            device_id=device, device_id_type=MESH)

    def inputs(h):
        pairs = ((q_hbm, q_ref), (k_hbm, k_ref), (v_hbm, v_ref), (g_hbm, g_ref))
        return [pltpu.make_async_copy(src.at[h], dst.at[h], in_sem.at[h, i]) for i, (src, dst) in enumerate(pairs)]

    def outputs(h, which):
        pairs = ((qg_ref, qg_hbm), (kg_ref, kg_hbm), (vg_ref, vg_hbm))
        return [pltpu.make_async_copy(pairs[i][0].at[h], pairs[i][1].at[h], out_sem.at[h, i]) for i in which]

    def first_half(i):
        return remote(loc.at[other + i], in_own.at[i], d_sem, (i,), mate)

    def second_half(i):
        return remote(loc.at[own + i, pl.ds(0, 2)], in_other.at[i], d_sem, (half + i,), mate)

    def f_copy(s, p):
        return remote(f_run.at[s, p], f_got.at[s, p], f_sem, (s, p), f_peer[s])

    def b_copy(s, p):
        return remote(b_msg.at[s, p], b_got.at[s, p], b_sem, (s, p), b_peer[s])

    def state_copy(s, p):
        return remote(st.at[s, own + p], st.at[s, own + p], s_sem, (s, p), mate)

    def grad_copy(p):
        return remote(gg.at[own + p], gg.at[own + p], t_sem, (p,), mate)

    def row_copy(i):
        return remote(slots.at[mine], slots.at[mine], w_sem, (i,), head_peers[i])

    def start_inputs(i, carry):
        for copy in inputs((other + i) % heads):
            copy.start()
        return carry

    lax.fori_loop(0, heads, start_inputs, 0)
    barrier = pltpu.get_barrier_semaphore()
    greeted = [mate, *f_peer, *head_peers]
    for device in greeted:
        pl.semaphore_signal(barrier, inc=1, device_id=device, device_id_type=MESH)
    w_all = jnp.concatenate([w_ref[...], w_ref[0 : 7 - levels, :]], axis=0)
    columns = w_all.T
    for row in range(levels + 1):
        wb[row] = jnp.broadcast_to(columns[:, row : row + 1], (length, dim))
    pl.semaphore_wait(barrier, len(greeted))

    def phase_one(h):
        for copy in inputs(h):
            copy.wait()
        g_f = g_ref[h].astype(F32)
        q_t = q_ref[h].T
        for pair in (1, 3):
            wide = jnp.concatenate([(wb[1 + pair + i] * g_f).astype(BF16) for i in range(2)], axis=1)
            both = mm(q_t, wide, 1, 0)
            loc[h, 1 + pair] = both[:, :dim]
            loc[h, 2 + pair] = both[:, dim:]
        kv = lower = None
        local = []
        for c in range(chunks):
            rows = parts[c]
            g_c = g_ref[h, rows].astype(F32)
            wide = jnp.concatenate([(wb[i, rows] * g_c).astype(BF16) for i in range(2)], axis=1)
            both = mm(q_t[:, c * CHUNK : (c + 1) * CHUNK], wide, 1, 0)
            local.append(both[:, :dim])
            lower = both[:, dim:] if c == 0 else lower + both[:, dim:]
            product = mm(k_ref[h, rows], v_ref[h, rows], 0, 0)
            kv = product if c == 0 else kv + product
            if c < chunks - 1:
                prefix[h, c] = kv.astype(BF16)
        loc[h, 0] = kv
        loc[h, 1] = lower
        total = None
        for c in range(chunks - 1, 0, -1):
            total = local[c] if total is None else total + local[c]
            suffix[h, c - 1] = total

    def level_sum(p, level):
        return loc[own + p, 1 + level] + in_own[p, 1 + level]

    def mate_part(i, carry):
        phase_one(other + i)
        first_half(i).start()
        return carry

    def own_part(i, carry):
        phase_one(own + i)
        second_half(i).start()
        first_half(i).wait_recv()
        b_msg[0, i] = bits[3] * level_sum(i, 4)
        b_copy(0, i).start()
        f_run[0, i] = loc[own + i, 0] + in_own[i, 0]
        f_copy(0, i).start()
        return carry

    lax.fori_loop(0, half, mate_part, 0)
    lax.fori_loop(0, half, own_part, 0)
    odd = flag(core == 1)
    for i in range(half):
        second_half(i).wait_recv()
        st0[own + i] = (odd * in_own[i, 0]).astype(BF16)
        st0[other + i] = (odd * in_other[i, 0]).astype(BF16)

    tri_row = lax.broadcasted_iota(jnp.int32, (CHUNK, CHUNK), 0)
    tri_col = lax.broadcasted_iota(jnp.int32, (CHUNK, CHUNK), 1)
    lower, upper = tri_row >= tri_col, tri_row <= tri_col

    def block(h, first):
        for c in (first, first + 1):
            rows = parts[c]
            q, k, v, g = (ref[h, rows] for ref in (q_ref, k_ref, v_ref, g_ref))
            w_0 = wb[0, rows]
            q_f = q.astype(F32)
            q_0 = (w_0 * q_f).astype(BF16)
            g_0 = (w_0 * g.astype(F32)).astype(BF16)
            raw_t = jnp.where(upper, mm(k, q, 1, 1), 0.0).astype(BF16)
            pv[h, rows] = mm(raw_t, g_0, 1, 0)
            da_t = jnp.where(upper, mm(v, g, 1, 1), 0.0).astype(BF16)
            pk[h, rows] = mm(da_t, q_0, 1, 0)
            da = jnp.where(lower, mm(g, v, 1, 1), 0.0).astype(BF16)
            z_0 = mm(da, k, 1, 0)
            if c:
                both = mm(g, jnp.concatenate([prefix[h, c - 1], st0[h]], axis=0), 1, 1)
                z_0, z_1 = z_0 + both[:, :dim], both[:, dim:]
            else:
                z_1 = mm(g, st0[h], 1, 1)
            tot[h, rows] = w_0 * z_0 + wb[1, rows] * z_1
            if h == 0:
                acc[0, rows] = q_f * z_0
                acc[1, rows] = q_f * z_1
            else:
                acc[0, rows] += q_f * z_0
                acc[1, rows] += q_f * z_1

    def level_pair(h, stage, fresh):
        both_states = jnp.concatenate([st[stage, h], st[stage + 1, h]], axis=0).astype(BF16)
        row = 2 + stage
        for rows in parts:
            both = mm(g_ref[h, rows], both_states, 1, 1)
            q_f = q_ref[h, rows].astype(F32)
            total = tot[h, rows]
            for i in range(2):
                z_i = both[:, i * dim : (i + 1) * dim]
                total = total + wb[row + i, rows] * z_i
                if fresh:
                    acc[row + i, rows] = q_f * z_i
                else:
                    acc[row + i, rows] += q_f * z_i
            if stage == 0:
                tot[h, rows] = total
            else:
                qg_ref[h, rows] = total.astype(BF16)
        if stage:
            for copy in outputs(h, (0,)):
                copy.start()

    def apply(h, grad_0):
        grad = gg[h] + flag(core == 0) * grad_0
        zero = jnp.zeros((dim, dim), BF16)
        for c, rows in enumerate(parts):
            x = (grad + suffix[h, c] if c < chunks - 1 else grad).astype(BF16)
            wide = jnp.concatenate([jnp.concatenate([x.T, zero], axis=1), jnp.concatenate([zero, x], axis=1)], axis=0)
            both = mm(jnp.concatenate([v_ref[h, rows], k_ref[h, rows]], axis=1), wide, 1, 0)
            kg_ref[h, rows] = (pk[h, rows] + both[:, :dim]).astype(BF16)
            vg_ref[h, rows] = (pv[h, rows] + both[:, dim:]).astype(BF16)
        for copy in outputs(h, (1, 2)):
            copy.start()

    def take_up(s, p):
        f_copy(s, p).wait_recv()
        got = f_got[s, p]
        if s < 3:
            f_run[s + 1, p] = f_run[s, p] + got
            f_copy(s + 1, p).start()
        st[s, own + p] = bits[s] * got
        state_copy(s, p).start()
        b_copy(s, p).wait_recv()
        total = b_got[s, p] if s == 0 else adj[p] + b_got[s, p]
        if s < 3:
            adj[p] = total
            b_msg[s + 1, p] = total + bits[2 - s] * level_sum(p, 3 - s)
            b_copy(s + 1, p).start()
        else:
            gg[own + p] = total
            grad_copy(p).start()

    work = [(h, c) for h in range(heads) for c in range(0, chunks, 2)]
    for _ in range(3):
        block(*work.pop(0))
    for s, p in ARRIVALS:
        take_up(s, p)
        if work:
            block(*work.pop(0))
        if s == 3:
            for stage in (0, 1):
                state_copy(stage, p).wait_recv()
            level_pair(own + p, 0, p == 0)
            level_pair(other + p, 0, False)
    while work:
        block(*work.pop(0))
    for p in range(half):
        level_pair(own + p, 2, p == 0)
    for p in range(half):
        for stage in (2, 3):
            state_copy(stage, p).wait_recv()
        level_pair(other + p, 2, False)
    ones = jnp.ones((8, dim), BF16)
    for row in range(levels + 1):
        term = acc[row]
        high = term.astype(BF16)
        low = (term - high.astype(F32)).astype(BF16)
        sums = mm(ones, high, 1, 1) + mm(ones, low, 1, 1)
        slots[mine, row : row + 1, :] = sums[0:1]
    for i in range(head_count - 1):
        row_copy(i).start()
    for p in range(half):
        apply(own + p, in_own[p, 1])
    for p in range(half):
        grad_copy(p).wait_recv()
        apply(other + p, in_other[p, 1])
    for i in range(head_count - 1):
        row_copy(i).wait_recv()
    total = slots[0]
    for index in range(1, head_count):
        total = total + slots[index]
    wg_ref[...] = total

    for i in range(half):
        first_half(i).wait_send()
        second_half(i).wait_send()
        grad_copy(i).wait_send()
    for s, p in ARRIVALS:
        f_copy(s, p).wait_send()
        b_copy(s, p).wait_send()
        state_copy(s, p).wait_send()
    for i in range(head_count - 1):
        row_copy(i).wait_send()
    for h in range(heads):
        for copy in outputs(h, (0, 1, 2)):
            copy.wait()


def per_device(queries, key_rows, value_rows, level_weight, out_grad):
    heads, length, dim = queries.shape
    half, rows = heads // 2, level_weight.shape[0]
    vmem, hbm = pl.BlockSpec(memory_space=pltpu.VMEM), pl.BlockSpec(memory_space=pl.ANY)

    def f32(*shape):
        return pltpu.VMEM(shape, F32)

    def square(*lead):
        return f32(*lead, dim, dim)

    def pairs(*shape):
        return pltpu.SemaphoreType.DMA((2, *shape))

    tokens = pltpu.VMEM((heads, length, dim), BF16)
    query_grad, key_grad, value_grad, weight_grad = pl.pallas_call(
        whole_kernel,
        in_specs=[hbm] * 4 + [vmem],
        out_specs=[hbm] * 3 + [vmem],
        out_shape=[jax.ShapeDtypeStruct(queries.shape, BF16)] * 3 + [jax.ShapeDtypeStruct(level_weight.shape, F32)],
        scratch_shapes=[tokens] * 7
        + [f32(heads, length, dim)] * 3
        + [f32(rows, length, dim)] * 2
        + [square(heads, 6), square(half, 6), square(half, 2)]
        + [square(4, half)] * 4
        + [square(half), pltpu.VMEM((heads, dim, dim), BF16), square(4, heads), square(heads)]
        + [pltpu.VMEM((heads, length // CHUNK - 1, dim, dim), BF16), square(heads, length // CHUNK - 1)]
        + [f32(4, rows, length)]
        + [pltpu.SemaphoreType.DMA((heads, 4)), pltpu.SemaphoreType.DMA((heads, 3))]
        + [pairs(heads), pairs(4, half), pairs(4, half), pairs(4, half), pairs(half), pairs(3)],
        compiler_params=pltpu.CompilerParams(
            collective_id=0, has_side_effects=True, vmem_limit_bytes=62 << 20),
    )(queries, key_rows, value_rows, out_grad, level_weight)
    return query_grad, key_grad, value_grad, weight_grad


def solution(mesh):
    rows = P("head", "ctx", None)
    return jax.shard_map(
        per_device,
        mesh=mesh,
        in_specs=(rows, rows, rows, P(None, "ctx"), rows),
        out_specs=(rows, rows, rows, P(None, "ctx")),
        check_vma=False,
    )
```

time: 301 us -> 51.6 us (0.17)
  matrix products: 129 us -> 0 us
  waiting for transfers between devices: 90.5 us -> 0 us
  Pallas kernels: 0 us -> 43.3 us
  local copies, waits for them, and re-layouts: 29.6 us -> 7.5 us
  blocking collectives: 17.7 us -> 0 us
  starting transfers between devices: 16.9 us -> 0 us
  other arithmetic: 14.2 us -> 0 us
    dot_general x53 -> x0, matrix products: 129 us -> none  [the longest x8 30.7 us: local_block(): jnp.einsum('ts,td->sd', attn, out_grad, preferred_element_type=jnp.float32)]
    ppermute x10 -> x0, waiting for transfers between devices: 90.5 us -> none  [partner_2(): lax.ppermute(shard, axis, [(i, i ^ 1 << distance) for i in range(lax.axis...]
    pallas_call x0 -> x1, Pallas kernels: none -> 43.3 us  [per_device(): pl.pallas_call(whole_kernel, in_specs=[hbm] * 4 + [vmem], out_specs=[hbm]...]
    psum x1 -> x0, blocking collectives: 17.7 us -> none  [per_device(): weight_grad = lax.psum(jnp.stack(weight_rows, axis=0), 'head')]
    ppermute x10 -> x0, starting transfers between devices: 16.9 us -> none  [partner_2(): lax.ppermute(shard, axis, [(i, i ^ 1 << distance) for i in range(lax.axis...]
    unnamed x37 -> x10, local copies, waits for them, and re-layouts: 21.6 us -> 7.5 us
    another operation x10 -> x0, other arithmetic: 9.24 us -> none  [the longest x7 9.24 us: per_device(): jnp.stack(pending[section_no:], axis=0)]
    slice x9 -> x0, local copies, waits for them, and re-layouts: 7.06 us -> none  [the longest x8 6.08 us: per_device(): level_weight[0]]
  transfers between devices with their start and end apart: 10 -> 0, of which waited for: 6 -> 0; matrix products, arithmetic and copies ran while one was open for 47% -> 0% of each run, Pallas kernels for 0% -> 0%
where the time goes in v3:
time: 51.6 us; the launch traced here: 51.4 us
  Pallas kernels  43.3 us (84%)
  local copies, waits for them, and re-layouts  7.5 us (15%)
  between operations  0.65 us (1%)
    pallas_call x1, Pallas kernels, per_device(): pl.pallas_call(whole_kernel, in_specs=[hbm] * 4 + [vmem], out_specs=[hbm]...  43.3 us
    unnamed x10, local copies, waits for them, and re-layouts  7.5 us

profile of v3, /device:TPU:0, one launch (start us, length us, event | category | flops | bytes accessed | tf_op | source)
XLA Modules:
  0.0 51.4 jit_solution(16645298039877855601)
XLA Ops:
  0.6 43.3 %shard_map.84 = (bf16[8,1024,128]{2,1,0:T(8,128)(2,1)}, bf16[8,1024,128]{2,1,0:T(8,128)(2,1)}, bf16[8,1024,128]{2,1,0:T(8,128)(2,1)}, f32[6,1024]{1,0:T(8,128)}) custom-call(bf16[8,1024,128]{2,1,0:T(8,128)(2,1)} %q_hbm.1, bf16[8,1024,128]{2,1,0:T(8,128)(2,1)} %k_hbm.1, bf16[8,1024,128]{2,1,0:T(8,128)(2,1)} %v_hbm.1, bf16[8,1024,128]{2,1,0:T(8,128)(2,1)} %g_hbm.1, ...), custom_call_target="tpu_custom_call" | custom-call | tf_op jit(solution)/shard_map/pallas_call | solution.py:307
  43.9 0.0 copy-start.1
  43.9 3.2 %copy.13 = bf16[8,1024,128]{2,1,0:T(8,128)(2,1)} copy(bf16[8,1024,128]{2,1,0:T(8,128)(2,1)} %get-tuple-element.8) | data formatting | bytes 4194304
  47.1 0.0 copy-done.1
  47.1 0.0 copy-start
  47.1 1.3 %copy.14 = bf16[8,1024,128]{2,1,0:T(8,128)(2,1)} copy(bf16[8,1024,128]{2,1,0:T(8,128)(2,1)S(1)} %copy-done.1) | data formatting | bytes 4194304
  48.5 1.0 %copy-done = bf16[8,1024,128]{2,1,0:T(8,128)(2,1)S(1)} copy-done((bf16[8,1024,128]{2,1,0:T(8,128)(2,1)S(1)}, bf16[8,1024,128]{2,1,0:T(8,128)(2,1)}, u32[]{:S(2)}) %copy-start) | copy-done | bytes 2097176
  49.5 0.0 copy-start.2
  49.5 1.3 %copy.15 = bf16[8,1024,128]{2,1,0:T(8,128)(2,1)} copy(bf16[8,1024,128]{2,1,0:T(8,128)(2,1)S(1)} %copy-done) | data formatting | bytes 4194304
  50.8 0.0 copy-done.2
  50.8 0.6 %copy.16 = f32[6,1024]{1,0:T(8,128)} copy(f32[6,1024]{1,0:T(8,128)S(1)} %copy-done.2) | data formatting | bytes 49152
Async XLA Ops:
  43.9 3.2 %copy-start.1 = (bf16[8,1024,128]{2,1,0:T(8,128)(2,1)S(1)}, bf16[8,1024,128]{2,1,0:T(8,128)(2,1)}, u32[]{:S(2)}) copy-start(bf16[8,1024,128]{2,1,0:T(8,128)(2,1)} %get-tuple-element.9) | copy-start | bytes 6291460
  47.1 2.3 %copy-start = (bf16[8,1024,128]{2,1,0:T(8,128)(2,1)S(1)}, bf16[8,1024,128]{2,1,0:T(8,128)(2,1)}, u32[]{:S(2)}) copy-start(bf16[8,1024,128]{2,1,0:T(8,128)(2,1)} %get-tuple-element.10) | copy-start | bytes 6291460
  49.5 1.3 %copy-start.2 = (f32[6,1024]{1,0:T(8,128)S(1)}, f32[6,1024]{1,0:T(8,128)}, u32[]{:S(2)}) copy-start(f32[6,1024]{1,0:T(8,128)} %get-tuple-element.11) | copy-start | bytes 73732

commit v4 on v3

--- a/solution.py
+++ b/solution.py
@@ -13,15 +13,18 @@
     (1, 3), (2, 1), (2, 2), (3, 0), (2, 3), (3, 1), (3, 2), (3, 3),
 )
 
+BLOCKS = (2, 1, 1, 1, 1, 1, 1, 1, 1, 1, 1, 0, 3, 0, 0, 0)
+MIDDLES = ((),) * 11 + ((0,), (), (1, 2), (3,), ())
+
 
 def mm(a, b, ca, cb):
     return lax.dot_general(a, b, (((ca,), (cb,)), ((), ())), preferred_element_type=F32)
 
 
-def whole_kernel(q_hbm, k_hbm, v_hbm, g_hbm, w_ref, qg_hbm, kg_hbm, vg_hbm, wg_ref,
-                 q_ref, k_ref, v_ref, g_ref, qg_ref, kg_ref, vg_ref, tot, pk, pv, wb, acc,
+def whole_kernel(q_hbm, k_hbm, v_hbm, g_hbm, w_ref, qg_ref, kg_ref, vg_ref, wg_ref,
+                 q_ref, k_ref, v_ref, g_ref, tot, pk, pv, wb, acc,
                  loc, in_own, in_other, f_run, f_got, b_msg, b_got, adj, st0, st, gg, prefix, suffix, slots,
-                 in_sem, out_sem, d_sem, f_sem, b_sem, s_sem, t_sem, w_sem):
+                 in_sem, d_sem, f_sem, b_sem, s_sem, t_sem, w_sem):
     me, mine = lax.axis_index("ctx"), lax.axis_index("head")
     core, z, y = me % 2, me // 2 % 4, me // 8
     heads, length, dim = q_ref.shape
@@ -53,15 +56,14 @@
         pairs = ((q_hbm, q_ref), (k_hbm, k_ref), (v_hbm, v_ref), (g_hbm, g_ref))
         return [pltpu.make_async_copy(src.at[h], dst.at[h], in_sem.at[h, i]) for i, (src, dst) in enumerate(pairs)]
 
-    def outputs(h, which):
-        pairs = ((qg_ref, qg_hbm), (kg_ref, kg_hbm), (vg_ref, vg_hbm))
-        return [pltpu.make_async_copy(pairs[i][0].at[h], pairs[i][1].at[h], out_sem.at[h, i]) for i in which]
-
-    def first_half(i):
-        return remote(loc.at[other + i], in_own.at[i], d_sem, (i,), mate)
-
-    def second_half(i):
-        return remote(loc.at[own + i, pl.ds(0, 2)], in_other.at[i], d_sem, (half + i,), mate)
+    def early_copy(i):
+        return remote(loc.at[other + i, pl.ds(0, 3)], in_own.at[i, pl.ds(0, 3)], d_sem, (i,), mate)
+
+    def late_copy(i):
+        return remote(loc.at[other + i, pl.ds(3, 3)], in_own.at[i, pl.ds(3, 3)], d_sem, (half + i,), mate)
+
+    def low_copy(i):
+        return remote(loc.at[own + i, pl.ds(2, 2)], in_other.at[i], d_sem, (2 * half + i,), mate)
 
     def f_copy(s, p):
         return remote(f_run.at[s, p], f_got.at[s, p], f_sem, (s, p), f_peer[s])
@@ -92,63 +94,85 @@
     columns = w_all.T
     for row in range(levels + 1):
         wb[row] = jnp.broadcast_to(columns[:, row : row + 1], (length, dim))
-    pl.semaphore_wait(barrier, len(greeted))
-
-    def phase_one(h):
+
+    def weighted_pair(h, rows, levels):
+        g_f = g_ref[h, rows].astype(F32)
+        return jnp.concatenate([(wb[level, rows] * g_f).astype(BF16) for level in levels], axis=1)
+
+    def upper_levels(h):
         for copy in inputs(h):
             copy.wait()
-        g_f = g_ref[h].astype(F32)
-        q_t = q_ref[h].T
-        for pair in (1, 3):
-            wide = jnp.concatenate([(wb[1 + pair + i] * g_f).astype(BF16) for i in range(2)], axis=1)
-            both = mm(q_t, wide, 1, 0)
-            loc[h, 1 + pair] = both[:, :dim]
-            loc[h, 2 + pair] = both[:, dim:]
-        kv = lower = None
-        local = []
-        for c in range(chunks):
-            rows = parts[c]
-            g_c = g_ref[h, rows].astype(F32)
-            wide = jnp.concatenate([(wb[i, rows] * g_c).astype(BF16) for i in range(2)], axis=1)
-            both = mm(q_t[:, c * CHUNK : (c + 1) * CHUNK], wide, 1, 0)
-            local.append(both[:, :dim])
-            lower = both[:, dim:] if c == 0 else lower + both[:, dim:]
+        both = mm(q_ref[h].T, weighted_pair(h, pl.ds(0, length), (4, 5)), 1, 0)
+        loc[h, 0] = both[:, :dim]
+        loc[h, 1] = both[:, dim:]
+        kv = None
+        for c, rows in enumerate(parts):
             product = mm(k_ref[h, rows], v_ref[h, rows], 0, 0)
             kv = product if c == 0 else kv + product
             if c < chunks - 1:
                 prefix[h, c] = kv.astype(BF16)
-        loc[h, 0] = kv
-        loc[h, 1] = lower
-        total = None
-        for c in range(chunks - 1, 0, -1):
-            total = local[c] if total is None else total + local[c]
-            suffix[h, c - 1] = total
+        loc[h, 2] = kv
+
+    def lower_levels(h):
+        q_t = q_ref[h].T
+        both = mm(q_t, weighted_pair(h, pl.ds(0, length), (2, 3)), 1, 0)
+        loc[h, 4] = both[:, :dim]
+        loc[h, 5] = both[:, dim:]
+        level_0 = total = None
+        for c in range(chunks - 1, -1, -1):
+            both = mm(q_t[:, c * CHUNK : (c + 1) * CHUNK], weighted_pair(h, parts[c], (0, 1)), 1, 0)
+            level_0 = both[:, dim:] if level_0 is None else level_0 + both[:, dim:]
+            if c:
+                total = both[:, :dim] if total is None else total + both[:, :dim]
+                suffix[h, c - 1] = total
+        loc[h, 3] = level_0
 
     def level_sum(p, level):
-        return loc[own + p, 1 + level] + in_own[p, 1 + level]
-
-    def mate_part(i, carry):
-        phase_one(other + i)
-        first_half(i).start()
-        return carry
-
-    def own_part(i, carry):
-        phase_one(own + i)
-        second_half(i).start()
-        first_half(i).wait_recv()
+        index = (3, 4, 5, 0, 1)[level]
+        return loc[own + p, index] + in_own[p, index]
+
+    def mate_early(i, carry):
+        upper_levels(other + i)
+        return carry
+
+    def mate_early_send(i, carry):
+        upper_levels(other + i)
+        early_copy(i).start()
+        return carry
+
+    def own_early(i, carry):
+        upper_levels(own + i)
+        early_copy(i).wait_recv()
         b_msg[0, i] = bits[3] * level_sum(i, 4)
         b_copy(0, i).start()
-        f_run[0, i] = loc[own + i, 0] + in_own[i, 0]
+        f_run[0, i] = loc[own + i, 2] + in_own[i, 2]
         f_copy(0, i).start()
         return carry
 
-    lax.fori_loop(0, half, mate_part, 0)
-    lax.fori_loop(0, half, own_part, 0)
+    def mate_late(i, carry):
+        lower_levels(other + i)
+        late_copy(i).start()
+        return carry
+
+    def own_late(i, carry):
+        lower_levels(own + i)
+        low_copy(i).start()
+        return carry
+
+    lax.fori_loop(0, 2, mate_early, 0)
+    pl.semaphore_wait(barrier, len(greeted))
+    for i in range(2):
+        early_copy(i).start()
+    lax.fori_loop(2, half, mate_early_send, 0)
+    lax.fori_loop(0, half, own_early, 0)
+    lax.fori_loop(0, half, mate_late, 0)
+    lax.fori_loop(0, half, own_late, 0)
     odd = flag(core == 1)
     for i in range(half):
-        second_half(i).wait_recv()
-        st0[own + i] = (odd * in_own[i, 0]).astype(BF16)
+        st0[own + i] = (odd * in_own[i, 2]).astype(BF16)
+        low_copy(i).wait_recv()
         st0[other + i] = (odd * in_other[i, 0]).astype(BF16)
+        late_copy(i).wait_recv()
 
     tri_row = lax.broadcasted_iota(jnp.int32, (CHUNK, CHUNK), 0)
     tri_col = lax.broadcasted_iota(jnp.int32, (CHUNK, CHUNK), 1)
@@ -199,9 +223,6 @@
                 tot[h, rows] = total
             else:
                 qg_ref[h, rows] = total.astype(BF16)
-        if stage:
-            for copy in outputs(h, (0,)):
-                copy.start()
 
     def apply(h, grad_0):
         grad = gg[h] + flag(core == 0) * grad_0
@@ -212,8 +233,6 @@
             both = mm(jnp.concatenate([v_ref[h, rows], k_ref[h, rows]], axis=1), wide, 1, 0)
             kg_ref[h, rows] = (pk[h, rows] + both[:, :dim]).astype(BF16)
             vg_ref[h, rows] = (pv[h, rows] + both[:, dim:]).astype(BF16)
-        for copy in outputs(h, (1, 2)):
-            copy.start()
 
     def take_up(s, p):
         f_copy(s, p).wait_recv()
@@ -233,20 +252,20 @@
             gg[own + p] = total
             grad_copy(p).start()
 
+    def middle(p):
+        for stage in (0, 1):
+            state_copy(stage, p).wait_recv()
+        level_pair(own + p, 0, p == 0)
+        level_pair(other + p, 0, False)
+
     work = [(h, c) for h in range(heads) for c in range(0, chunks, 2)]
-    for _ in range(3):
-        block(*work.pop(0))
-    for s, p in ARRIVALS:
+    block(*work.pop(0))
+    for index, (s, p) in enumerate(ARRIVALS):
         take_up(s, p)
-        if work:
+        for _ in range(BLOCKS[index]):
             block(*work.pop(0))
-        if s == 3:
-            for stage in (0, 1):
-                state_copy(stage, p).wait_recv()
-            level_pair(own + p, 0, p == 0)
-            level_pair(other + p, 0, False)
-    while work:
-        block(*work.pop(0))
+        for piece in MIDDLES[index]:
+            middle(piece)
     for p in range(half):
         level_pair(own + p, 2, p == 0)
     for p in range(half):
@@ -263,7 +282,7 @@
     for i in range(head_count - 1):
         row_copy(i).start()
     for p in range(half):
-        apply(own + p, in_own[p, 1])
+        apply(own + p, in_own[p, 3])
     for p in range(half):
         grad_copy(p).wait_recv()
         apply(other + p, in_other[p, 1])
@@ -275,8 +294,9 @@
     wg_ref[...] = total
 
     for i in range(half):
-        first_half(i).wait_send()
-        second_half(i).wait_send()
+        early_copy(i).wait_send()
+        late_copy(i).wait_send()
+        low_copy(i).wait_send()
         grad_copy(i).wait_send()
     for s, p in ARRIVALS:
         f_copy(s, p).wait_send()
@@ -284,15 +304,33 @@
         state_copy(s, p).wait_send()
     for i in range(head_count - 1):
         row_copy(i).wait_send()
-    for h in range(heads):
-        for copy in outputs(h, (0, 1, 2)):
-            copy.wait()
+
+
+def copy_out_kernel(*refs):
+    count = len(refs) // 2
+    sems = refs[-1]
+    copies = [pltpu.make_async_copy(refs[i], refs[count + i], sems.at[i]) for i in range(count)]
+    for copy in copies:
+        copy.start()
+    for copy in copies:
+        copy.wait()
+
+
+def copy_out(arrays):
+    return pl.pallas_call(
+        copy_out_kernel,
+        in_specs=[pl.BlockSpec(memory_space=pltpu.VMEM)] * len(arrays),
+        out_specs=[pl.BlockSpec(memory_space=pl.ANY)] * len(arrays),
+        out_shape=[jax.ShapeDtypeStruct(array.shape, array.dtype) for array in arrays],
+        scratch_shapes=[pltpu.SemaphoreType.DMA((len(arrays),))],
+        compiler_params=pltpu.CompilerParams(vmem_limit_bytes=1 << 20),
+    )(*arrays)
 
 
 def per_device(queries, key_rows, value_rows, level_weight, out_grad):
     heads, length, dim = queries.shape
     half, rows = heads // 2, level_weight.shape[0]
-    vmem, hbm = pl.BlockSpec(memory_space=pltpu.VMEM), pl.BlockSpec(memory_space=pl.ANY)
+    vmem, hbm = pl.BlockSpec(memory_space=pltpu.VMEM), pl.BlockSpec(memory_space=pltpu.HBM)
 
     def f32(*shape):
         return pltpu.VMEM(shape, F32)
@@ -304,12 +342,12 @@
         return pltpu.SemaphoreType.DMA((2, *shape))
 
     tokens = pltpu.VMEM((heads, length, dim), BF16)
-    query_grad, key_grad, value_grad, weight_grad = pl.pallas_call(
+    arrays = pl.pallas_call(
         whole_kernel,
         in_specs=[hbm] * 4 + [vmem],
-        out_specs=[hbm] * 3 + [vmem],
+        out_specs=[vmem] * 4,
         out_shape=[jax.ShapeDtypeStruct(queries.shape, BF16)] * 3 + [jax.ShapeDtypeStruct(level_weight.shape, F32)],
-        scratch_shapes=[tokens] * 7
+        scratch_shapes=[tokens] * 4
         + [f32(heads, length, dim)] * 3
         + [f32(rows, length, dim)] * 2
         + [square(heads, 6), square(half, 6), square(half, 2)]
@@ -317,12 +355,12 @@
         + [square(half), pltpu.VMEM((heads, dim, dim), BF16), square(4, heads), square(heads)]
         + [pltpu.VMEM((heads, length // CHUNK - 1, dim, dim), BF16), square(heads, length // CHUNK - 1)]
         + [f32(4, rows, length)]
-        + [pltpu.SemaphoreType.DMA((heads, 4)), pltpu.SemaphoreType.DMA((heads, 3))]
-        + [pairs(heads), pairs(4, half), pairs(4, half), pairs(4, half), pairs(half), pairs(3)],
+        + [pltpu.SemaphoreType.DMA((heads, 4))]
+        + [pairs(3 * half), pairs(4, half), pairs(4, half), pairs(4, half), pairs(half), pairs(3)],
         compiler_params=pltpu.CompilerParams(
-            collective_id=0, has_side_effects=True, vmem_limit_bytes=62 << 20),
+            collective_id=0, has_side_effects=True, vmem_limit_bytes=44 << 20),
     )(queries, key_rows, value_rows, out_grad, level_weight)
-    return query_grad, key_grad, value_grad, weight_grad
+    return tuple(copy_out(arrays))
 
 
 def solution(mesh):

time: 51.6 us -> 47.4 us (0.919)
  local copies, waits for them, and re-layouts: 7.5 us -> 2.34 us
  Pallas kernels: 43.3 us -> 44 us
    unnamed x10 -> x4, local copies, waits for them, and re-layouts: 7.5 us -> 2.34 us
    pallas_call x1 -> x2, Pallas kernels: 43.3 us -> 44 us  [the longest x1 41.3 us: per_device(): pl.pallas_call(whole_kernel, in_specs=[hbm] * 4 + [vmem], out_specs=[vmem...]
where the time goes in v4:
time: 47.4 us; the launch traced here: 47.2 us
  Pallas kernels  44 us (93%)
  local copies, waits for them, and re-layouts  2.34 us (5%)
  between operations  0.83 us (2%)
    pallas_call x1, Pallas kernels, per_device(): pl.pallas_call(whole_kernel, in_specs=[hbm] * 4 + [vmem], out_specs=[vmem...  41.3 us
    pallas_call x1, Pallas kernels, copy_out(): pl.pallas_call(copy_out_kernel, in_specs=[pl.BlockSpec(memory_space=pltpu...  2.74 us
    unnamed x4, local copies, waits for them, and re-layouts  2.34 us

profile of v4, /device:TPU:0, one launch (start us, length us, event | category | flops | bytes accessed | tf_op | source)
XLA Modules:
  0.0 47.2 jit_solution(4178502944000035656)
XLA Ops:
  0.6 0.0 copy-start
  0.6 1.6 %copy-done = bf16[8,1024,128]{2,1,0:T(8,128)(2,1)S(1)} copy-done((bf16[8,1024,128]{2,1,0:T(8,128)(2,1)S(1)}, bf16[8,1024,128]{2,1,0:T(8,128)(2,1)}, u32[]{:S(2)}) %copy-start) | copy-done | bytes 2097176
  2.2 0.0 copy-start.1
  2.2 0.8 %copy-done.1 = f32[6,1024]{1,0:T(8,128)S(1)} copy-done((f32[6,1024]{1,0:T(8,128)S(1)}, f32[6,1024]{1,0:T(8,128)}, u32[]{:S(2)}) %copy-start.1) | copy-done | bytes 24600
  3.0 41.3 %shard_map.84 = (bf16[8,1024,128]{2,1,0:T(8,128)(2,1)S(1)}, bf16[8,1024,128]{2,1,0:T(8,128)(2,1)S(1)}, bf16[8,1024,128]{2,1,0:T(8,128)(2,1)S(1)}, f32[6,1024]{1,0:T(8,128)S(1)}) custom-call(bf16[8,1024,128]{2,1,0:T(8,128)(2,1)S(1)} %copy-done, bf16[8,1024,128]{2,1,0:T(8,128)(2,1)} %k_hbm.1, bf16[8,1024,128]{2,1,0:T(8,128)(2,1)} %v_hbm.1, ...), custom_call_target="tpu_custom_call" | custom-call | tf_op jit(solution)/shard_map/pallas_call | solution.py:345
  44.3 2.7 %shard_map.85 = (bf16[8,1024,128]{2,1,0:T(8,128)(2,1)}, bf16[8,1024,128]{2,1,0:T(8,128)(2,1)}, bf16[8,1024,128]{2,1,0:T(8,128)(2,1)}, f32[6,1024]{1,0:T(8,128)}) custom-call(bf16[8,1024,128]{2,1,0:T(8,128)(2,1)S(1)} %get-tuple-element.8.refs_0_, bf16[8,1024,128]{2,1,0:T(8,128)(2,1)S(1)} %get-tuple-element.9.refs_1_, ...), custom_call_target="tpu_custom_call" | custom-call | tf_op jit(solution)/shard_map/pallas_call | solution.py:320
Async XLA Ops:
  0.6 1.6 %copy-start = (bf16[8,1024,128]{2,1,0:T(8,128)(2,1)S(1)}, bf16[8,1024,128]{2,1,0:T(8,128)(2,1)}, u32[]{:S(2)}) copy-start(bf16[8,1024,128]{2,1,0:T(8,128)(2,1)} %q_hbm.1) | copy-start | bytes 6291460
  2.2 0.8 %copy-start.1 = (f32[6,1024]{1,0:T(8,128)S(1)}, f32[6,1024]{1,0:T(8,128)}, u32[]{:S(2)}) copy-start(f32[6,1024]{1,0:T(8,128)} %w_ref.1) | copy-start | bytes 73732

commit v5 on v4

--- a/solution.py
+++ b/solution.py
@@ -190,8 +190,7 @@
             pv[h, rows] = mm(raw_t, g_0, 1, 0)
             da_t = jnp.where(upper, mm(v, g, 1, 1), 0.0).astype(BF16)
             pk[h, rows] = mm(da_t, q_0, 1, 0)
-            da = jnp.where(lower, mm(g, v, 1, 1), 0.0).astype(BF16)
-            z_0 = mm(da, k, 1, 0)
+            z_0 = mm(da_t, k, 0, 0)
             if c:
                 both = mm(g, jnp.concatenate([prefix[h, c - 1], st0[h]], axis=0), 1, 1)
                 z_0, z_1 = z_0 + both[:, :dim], both[:, dim:]
@@ -358,7 +357,7 @@
         + [pltpu.SemaphoreType.DMA((heads, 4))]
         + [pairs(3 * half), pairs(4, half), pairs(4, half), pairs(4, half), pairs(half), pairs(3)],
         compiler_params=pltpu.CompilerParams(
-            collective_id=0, has_side_effects=True, vmem_limit_bytes=44 << 20),
+            collective_id=0, has_side_effects=True, vmem_limit_bytes=47 << 20),
     )(queries, key_rows, value_rows, out_grad, level_weight)
     return tuple(copy_out(arrays))
 

time: 47.4 us -> 45.4 us (0.958)
  local copies, waits for them, and re-layouts: 2.34 us -> 0.75 us
    unnamed x4 -> x2, local copies, waits for them, and re-layouts: 2.34 us -> 0.75 us
where the time goes in v5:
time: 45.4 us; the launch traced here: 45.2 us
  Pallas kernels  43.6 us (96%)
  between operations  0.83 us (2%)
  local copies, waits for them, and re-layouts  0.75 us (2%)
    pallas_call x1, Pallas kernels, per_device(): pl.pallas_call(whole_kernel, in_specs=[hbm] * 4 + [vmem], out_specs=[vmem...  40.9 us
    pallas_call x1, Pallas kernels, copy_out(): pl.pallas_call(copy_out_kernel, in_specs=[pl.BlockSpec(memory_space=pltpu...  2.74 us

profile of v5, /device:TPU:0, one launch (start us, length us, event | category | flops | bytes accessed | tf_op | source)
XLA Modules:
  0.0 45.2 jit_solution(3362136194083486315)
XLA Ops:
  0.6 0.0 copy-start
  0.6 0.7 %copy-done = f32[6,1024]{1,0:T(8,128)S(1)} copy-done((f32[6,1024]{1,0:T(8,128)S(1)}, f32[6,1024]{1,0:T(8,128)}, u32[]{:S(2)}) %copy-start) | copy-done | bytes 24600
  1.4 40.9 %shard_map.84 = (bf16[8,1024,128]{2,1,0:T(8,128)(2,1)S(1)}, bf16[8,1024,128]{2,1,0:T(8,128)(2,1)S(1)}, bf16[8,1024,128]{2,1,0:T(8,128)(2,1)S(1)}, f32[6,1024]{1,0:T(8,128)S(1)}) custom-call(bf16[8,1024,128]{2,1,0:T(8,128)(2,1)} %q_hbm.1, bf16[8,1024,128]{2,1,0:T(8,128)(2,1)} %k_hbm.1, bf16[8,1024,128]{2,1,0:T(8,128)(2,1)} %v_hbm.1, ...), custom_call_target="tpu_custom_call" | custom-call | tf_op jit(solution)/shard_map/pallas_call | solution.py:344
  42.3 2.7 %shard_map.85 = (bf16[8,1024,128]{2,1,0:T(8,128)(2,1)}, bf16[8,1024,128]{2,1,0:T(8,128)(2,1)}, bf16[8,1024,128]{2,1,0:T(8,128)(2,1)}, f32[6,1024]{1,0:T(8,128)}) custom-call(bf16[8,1024,128]{2,1,0:T(8,128)(2,1)S(1)} %get-tuple-element.8.refs_0_, bf16[8,1024,128]{2,1,0:T(8,128)(2,1)S(1)} %get-tuple-element.9.refs_1_, ...), custom_call_target="tpu_custom_call" | custom-call | tf_op jit(solution)/shard_map/pallas_call | solution.py:319
Async XLA Ops:
  0.6 0.8 %copy-start = (f32[6,1024]{1,0:T(8,128)S(1)}, f32[6,1024]{1,0:T(8,128)}, u32[]{:S(2)}) copy-start(f32[6,1024]{1,0:T(8,128)} %w_ref.1) | copy-start | bytes 73732
